TPU v7x, 256 devices: a whole 4x4x8 slice. The times are simulated.
256 devices in a mesh: grp: 16 (over y_hi, x, core), sub: 16 (over y_lo, z).
Axes of the slice: x: 4, y: 4 (y_hi: 2, y_lo: 2; y = y_hi * 2 + y_lo), z: 8, core: 2. Of those that a mesh axis runs over, the one named last changes fastest.
Arguments:
- arrivals: float32 [128, 262144], P('sub', 'grp'), may hold values from -64 to 64
- sketch: float32 [256, 262144], P(None, ('grp', 'sub')), may hold values from -96 to 96
- owner: int32 [8192], P('grp'), may hold values from 0 to 511, as said below
- slot: int32 [128], replicated, may hold values from 0 to 127, each once
Outputs:
- final_sketch: float32 [256, 262144], P(None, ('grp', 'sub'))
- residual: float32 [128, 262144], P(None, ('grp', 'sub'))
Inputs may be any that keep to these rules, and one draw needn't show every extreme that they name: `owner`: each aligned block of 512 entries names each host of its group once. `slot`: each time step has its own arrival row.
All inputs are finite; a program needn't handle non-finite values.
Results may differ from a plain program's by a relative error of at most 0.00016.
Values sent between devices are 32-bit elements; how exact they have to be, the bound alone decides.
A program may use at most 64 MiB of HBM per device.

v0:
```python
import jax
import jax.numpy as jnp
from jax import lax
from jax.sharding import Mesh
from jax.sharding import PartitionSpec as P

ELL = 256
NEW = 64
TOP = 32
ROWS = 320
SUB = ("sub_0", "sub_1")
GRP_SUB = ("grp_0", "grp_1", "grp_2", "sub_0", "sub_1")
GRP = ("grp_0", "grp_1", "grp_2")


highest = lax.Precision.HIGHEST


def one_axis_at_a_time(x, axes):
    for axis in axes:
        x = lax.psum(x, axis)
    return x


def product(former, latter):
    return jnp.dot(former, latter, precision=highest, preferred_element_type=jnp.float32)


def symmetric(matrix):
    return 0.5 * (matrix + matrix.T)


def lower_inverse(triangle):
    identity = jnp.eye(triangle.shape[0], dtype=jnp.float32)
    return jax.scipy.linalg.solve_triangular(triangle, identity, lower=True)


def orthonormal(columns):
    factor = jnp.linalg.cholesky(symmetric(product(columns.T, columns)))
    return jax.scipy.linalg.solve_triangular(factor, columns.T, lower=True).T


def shrink_factors(gram_matrix):
    subspace = orthonormal(gram_matrix[:, :ELL])
    reduced = symmetric(product(subspace.T, product(gram_matrix, subspace)))
    inverse_root = lower_inverse(jnp.linalg.cholesky(reduced))
    offset = 0.5 / jnp.sum(inverse_root * inverse_root)
    keeper = jnp.eye(ELL, dtype=jnp.float32) - offset * product(inverse_root.T, inverse_root)
    shrink_factor = jnp.linalg.cholesky(symmetric(keeper)).T
    return (product(shrink_factor, subspace.T), shrink_factor, reduced)


def local(arrivals, sketch, owner, slot):
    arrived_rows, arrived_columns = arrivals.shape
    host_count = owner.shape[0]
    shaped = arrivals.reshape(arrived_rows, host_count, arrived_columns // host_count)
    placed = jnp.take(shaped, owner, axis=1).reshape(arrived_rows, arrived_columns)
    regrouped = lax.all_to_all(placed, SUB, split_axis=1, concat_axis=0, tiled=True)
    samples = jnp.take(regrouped, slot, axis=0)
    first_batch = samples[:NEW]
    second_batch = samples[NEW:]
    stacked = jnp.concatenate([sketch, first_batch], axis=0)
    gram_one = lax.psum(product(stacked, stacked.T), GRP_SUB)
    weights_one, factor_one, reduced_one = shrink_factors(gram_one)
    middle = product(weights_one, stacked)
    stacked_two = jnp.concatenate([middle, second_batch], axis=0)
    extended = jnp.concatenate([stacked_two, first_batch], axis=0)
    summed = one_axis_at_a_time(product(extended, second_batch.T), GRP_SUB)
    corner = symmetric(product(factor_one, product(reduced_one, factor_one.T)))
    side_block = summed[:ROWS]
    upper_rows = jnp.concatenate([corner, side_block[:ELL]], axis=1)
    gram_two = jnp.concatenate([upper_rows, side_block.T], axis=0)
    early_rows = jnp.concatenate([product(gram_one[ELL:], weights_one.T), summed[ROWS:]], axis=1)
    weights_two, factor_two, reduced_two = shrink_factors(gram_two)
    final_sketch = product(weights_two, stacked_two)
    spectrum = symmetric(product(factor_two, product(reduced_two, factor_two.T)))
    leading = orthonormal(spectrum[:, :TOP])
    directions = product(leading.T, final_sketch)
    small_gram = symmetric(product(leading.T, product(spectrum, leading)))
    inverse_root = lower_inverse(jnp.linalg.cholesky(small_gram))
    sample_rows = jnp.concatenate([early_rows, gram_two[ELL:]], axis=0)
    scores = product(sample_rows, product(weights_two.T, leading))
    coefficients = product(product(scores, inverse_root.T), inverse_root)
    residual = samples - product(coefficients, directions)
    return (final_sketch, residual)


def solution(mesh):
    split = Mesh(mesh.devices.reshape(2, 4, 2, 2, 8), ("grp_0", "grp_1", "grp_2", "sub_0", "sub_1"))
    placed = (P(SUB, GRP), P(None, GRP_SUB), P(GRP), P())
    return jax.shard_map(
        local,
        mesh=split,
        in_specs=placed,
        out_specs=(P(None, GRP_SUB), P(None, GRP_SUB)),
        check_vma=False,
    )
```

profile of v0, /device:TPU:1, one launch (start us, length us, event | category | flops | bytes accessed | tf_op | source)
XLA Modules:
  0.0 895.4 jit_solution(13229806428466531764)
XLA Ops:
  21.2 10.1 %all-to-all-start = ((f32[8,16,1024]{2,0,1:T(8,128)}), f32[8,16,1024]{2,0,1:T(8,128)S(1)}, u32[]{:S(2)}, u32[]{:S(2)}) async-start(f32[8,16,1024]{2,0,1:T(8,128)} %copy.55), calls=%async_computation | async-start | bytes 1048576 | tf_op jit(solution)/shard_map/all_to_all | solution.py:58
  31.6 13.5 %all-to-all-done = f32[8,16,1024]{2,0,1:T(8,128)S(1)} async-done(((f32[8,16,1024]{2,0,1:T(8,128)}), f32[8,16,1024]{2,0,1:T(8,128)S(1)}, u32[]{:S(2)}, u32[]{:S(2)}) %all-to-all-start) | async-done | bytes 524320 | tf_op jit(solution)/shard_map/all_to_all | solution.py:58
  50.6 253.8 %all-reduce.8.cloned.1.call-done = f32[320,320]{1,0:T(8,128)} async-done(((f32[320,320]{1,0:T(8,128)}), f32[320,320]{1,0:T(8,128)}) %all-reduce.8.cloned.1.call-update) | async-done | bytes 409616 | tf_op jit(solution)/shard_map/psum | solution.py:63
  306.8 11.7 %cholesky.340 = f32[128,128]{1,0:T(8,128)S(1)} custom-call(f32[128,128]{1,0:T(8,128)S(1)} %cholesky.562), custom_call_target="Cholesky" | custom-call | tf_op jit(solution)/shard_map/jit(cholesky)/cholesky | solution.py:39
  318.5 9.8 %custom-call.33 = f32[1,128,128]{1,2,0:T(8,128)S(1)} custom-call(f32[1,128,128]{2,1,0:T(8,128)S(1)} %get-tuple-element.103), custom_call_target="InvertDiagBlocksLowerTriangular" | custom-call | tf_op jit(solution)/shard_map/jit(cholesky)/cholesky | solution.py:39
  328.9 11.7 %cholesky.357 = f32[128,128]{1,0:T(8,128)S(1)} custom-call(f32[128,128]{1,0:T(8,128)S(1)} %convolution_subtract_fusion.10), custom_call_target="Cholesky" | custom-call | tf_op jit(solution)/shard_map/jit(cholesky)/cholesky | solution.py:39
  346.4 20.1 %custom-call.34 = f32[2,128,128]{1,2,0:T(8,128)S(1)} custom-call(f32[2,128,128]{2,1,0:T(8,128)S(1)} %get-tuple-element.34), custom_call_target="InvertDiagBlocksLowerTriangular" | custom-call | tf_op jit(solution)/shard_map/jit(_solve_triangular)/triangular_solve | solution.py:40
  369.4 11.7 %cholesky.374 = f32[128,128]{1,0:T(8,128)S(1)} custom-call(f32[128,128]{1,0:T(8,128)S(1)} %cholesky.565), custom_call_target="Cholesky" | custom-call | tf_op jit(solution)/shard_map/jit(cholesky)/cholesky | solution.py:46
  381.2 9.8 %custom-call.35 = f32[1,128,128]{1,2,0:T(8,128)S(1)} custom-call(f32[1,128,128]{2,1,0:T(8,128)S(1)} %get-tuple-element.99), custom_call_target="InvertDiagBlocksLowerTriangular" | custom-call | tf_op jit(solution)/shard_map/jit(cholesky)/cholesky | solution.py:46
  391.5 11.9 %cholesky.391 = f32[128,128]{1,0:T(8,128)S(1)} custom-call(f32[128,128]{1,0:T(8,128)S(1)} %convolution_subtract_fusion.9), custom_call_target="Cholesky" | custom-call | tf_op jit(solution)/shard_map/jit(cholesky)/cholesky | solution.py:46
  406.2 4.1 while.9
  410.3 19.7 %custom-call.36 = f32[2,128,128]{1,2,0:T(8,128)S(1)} custom-call(f32[2,128,128]{2,1,0:T(8,128)S(1)} %get-tuple-element.35), custom_call_target="InvertDiagBlocksLowerTriangular" | custom-call | tf_op jit(solution)/shard_map/jit(_solve_triangular)/triangular_solve | solution.py:35
  433.2 11.7 %cholesky.408 = f32[128,128]{1,0:T(8,128)S(1)} custom-call(f32[128,128]{1,0:T(8,128)S(1)} %cholesky.568), custom_call_target="Cholesky" | custom-call | tf_op jit(solution)/shard_map/jit(cholesky)/cholesky | solution.py:49
  445.0 9.8 %custom-call.37 = f32[1,128,128]{1,2,0:T(8,128)S(1)} custom-call(f32[1,128,128]{2,1,0:T(8,128)S(1)} %get-tuple-element.95), custom_call_target="InvertDiagBlocksLowerTriangular" | custom-call | tf_op jit(solution)/shard_map/jit(cholesky)/cholesky | solution.py:49
  455.3 11.7 %cholesky.425 = f32[128,128]{1,0:T(8,128)S(1)} custom-call(f32[128,128]{1,0:T(8,128)S(1)} %convolution_subtract_fusion.8), custom_call_target="Cholesky" | custom-call | tf_op jit(solution)/shard_map/jit(cholesky)/cholesky | solution.py:49
  475.9 33.5 %all-reduce.10.cloned.1.call-done = f32[384,64]{0,1:T(8,128)} async-done(((f32[384,64]{0,1:T(8,128)}), f32[384,64]{0,1:T(8,128)}) %all-reduce.10.cloned.1.call-update) | async-done | bytes 98320 | tf_op jit(solution)/shard_map/psum | solution.py:21
  510.1 45.9 %all-reduce.12.cloned.1.call-done = f32[384,64]{0,1:T(8,128)} async-done(((f32[384,64]{0,1:T(8,128)}), f32[384,64]{0,1:T(8,128)}) %all-reduce.12.cloned.1.call-update) | async-done | bytes 98320 | tf_op jit(solution)/shard_map/psum | solution.py:21
  556.7 33.6 %all-reduce.14.cloned.1.call-done = f32[384,64]{0,1:T(8,128)} async-done(((f32[384,64]{0,1:T(8,128)}), f32[384,64]{0,1:T(8,128)}) %all-reduce.14.cloned.1.call-update) | async-done | bytes 98320 | tf_op jit(solution)/shard_map/psum | solution.py:21
  590.4 35.4 %all-reduce.16.cloned.1.call-done = f32[384,64]{0,1:T(8,128)} async-done(((f32[384,64]{0,1:T(8,128)}), f32[384,64]{0,1:T(8,128)}) %all-reduce.16.cloned.1.call-update) | async-done | bytes 98320 | tf_op jit(solution)/shard_map/psum | solution.py:21
  628.1 68.7 %all-reduce.18.cloned.1.call-done = f32[384,64]{0,1:T(8,128)} async-done(((f32[384,64]{0,1:T(8,128)}), f32[384,64]{0,1:T(8,128)}) %all-reduce.18.cloned.1.call-update) | async-done | bytes 98320 | tf_op jit(solution)/shard_map/psum | solution.py:21
  699.7 11.7 %cholesky.442 = f32[128,128]{1,0:T(8,128)S(1)} custom-call(f32[128,128]{1,0:T(8,128)S(1)} %cholesky.571), custom_call_target="Cholesky" | custom-call | tf_op jit(solution)/shard_map/jit(cholesky)/cholesky | solution.py:39
  711.5 9.8 %custom-call.38 = f32[1,128,128]{1,2,0:T(8,128)S(1)} custom-call(f32[1,128,128]{2,1,0:T(8,128)S(1)} %get-tuple-element.91), custom_call_target="InvertDiagBlocksLowerTriangular" | custom-call | tf_op jit(solution)/shard_map/jit(cholesky)/cholesky | solution.py:39
  721.8 11.7 %cholesky.459 = f32[128,128]{1,0:T(8,128)S(1)} custom-call(f32[128,128]{1,0:T(8,128)S(1)} %convolution_subtract_fusion.7), custom_call_target="Cholesky" | custom-call | tf_op jit(solution)/shard_map/jit(cholesky)/cholesky | solution.py:39
  736.3 4.1 while.10
  740.4 19.8 %custom-call.39 = f32[2,128,128]{1,2,0:T(8,128)S(1)} custom-call(f32[2,128,128]{2,1,0:T(8,128)S(1)} %get-tuple-element.36), custom_call_target="InvertDiagBlocksLowerTriangular" | custom-call | tf_op jit(solution)/shard_map/jit(_solve_triangular)/triangular_solve | solution.py:40
  763.8 11.7 %cholesky.476 = f32[128,128]{1,0:T(8,128)S(1)} custom-call(f32[128,128]{1,0:T(8,128)S(1)} %cholesky.574), custom_call_target="Cholesky" | custom-call | tf_op jit(solution)/shard_map/jit(cholesky)/cholesky | solution.py:46
  775.6 9.8 %custom-call.40 = f32[1,128,128]{1,2,0:T(8,128)S(1)} custom-call(f32[1,128,128]{2,1,0:T(8,128)S(1)} %get-tuple-element.87), custom_call_target="InvertDiagBlocksLowerTriangular" | custom-call | tf_op jit(solution)/shard_map/jit(cholesky)/cholesky | solution.py:46
  785.9 11.9 %cholesky.493 = f32[128,128]{1,0:T(8,128)S(1)} custom-call(f32[128,128]{1,0:T(8,128)S(1)} %convolution_subtract_fusion.6), custom_call_target="Cholesky" | custom-call | tf_op jit(solution)/shard_map/jit(cholesky)/cholesky | solution.py:46
  804.5 19.7 %custom-call.41 = f32[2,128,128]{1,2,0:T(8,128)S(1)} custom-call(f32[2,128,128]{2,1,0:T(8,128)S(1)} %get-tuple-element.37), custom_call_target="InvertDiagBlocksLowerTriangular" | custom-call | tf_op jit(solution)/shard_map/jit(_solve_triangular)/triangular_solve | solution.py:35
  827.7 11.7 %cholesky.510 = f32[128,128]{1,0:T(8,128)S(1)} custom-call(f32[128,128]{1,0:T(8,128)S(1)} %cholesky.577), custom_call_target="Cholesky" | custom-call | tf_op jit(solution)/shard_map/jit(cholesky)/cholesky | solution.py:49
  839.5 9.8 %custom-call.42 = f32[1,128,128]{1,2,0:T(8,128)S(1)} custom-call(f32[1,128,128]{2,1,0:T(8,128)S(1)} %get-tuple-element.83), custom_call_target="InvertDiagBlocksLowerTriangular" | custom-call | tf_op jit(solution)/shard_map/jit(cholesky)/cholesky | solution.py:49
  849.8 11.7 %cholesky.527 = f32[128,128]{1,0:T(8,128)S(1)} custom-call(f32[128,128]{1,0:T(8,128)S(1)} %convolution_subtract_fusion.5), custom_call_target="Cholesky" | custom-call | tf_op jit(solution)/shard_map/jit(cholesky)/cholesky | solution.py:49
  (234 shorter events, 104.6 us)
Async XLA Ops:
  20.1 11.5 %copy-start.9 = (s32[128]{0:T(128)S(1)}, s32[128]{0:T(128)}, u32[]{:S(2)}) copy-start(s32[128]{0:T(128)} %param.13) | copy-start | bytes 1540
  21.2 23.9 %all-to-all-start = ((f32[8,16,1024]{2,0,1:T(8,128)}), f32[8,16,1024]{2,0,1:T(8,128)S(1)}, u32[]{:S(2)}, u32[]{:S(2)}) async-start(f32[8,16,1024]{2,0,1:T(8,128)} %copy.55), calls=%async_computation | async-start | bytes 1048576 | tf_op jit(solution)/shard_map/all_to_all | solution.py:58
  31.4 273.1 %all-reduce.8.cloned.1.call-start = ((), (), s32[]{:S(2)}) async-start(), calls=%async_computation.1 | async-start | bytes 983040 | tf_op jit(solution)/shard_map/psum | solution.py:63
  46.0 1.3 copy-start
  46.8 259.6 %copy-start.5 = (f32[64,1024]{1,0:T(8,128)}, f32[64,1024]{1,0:T(8,128)S(1)}, u32[]{:S(2)}) copy-start(f32[64,1024]{1,0:T(8,128)S(1)} %get-tuple-element.78) | copy-start | bytes 786436
  50.3 459.1 %all-reduce.10.cloned.1.call-start = ((), (), s32[]{:S(2)}) async-start(), calls=%async_computation.2 | async-start | bytes 196608 | tf_op jit(solution)/shard_map/psum | solution.py:21
  50.6 379.7 %copy-start.3 = (f32[256,256]{1,0:T(8,128)}, f32[256,256]{1,0:T(8,128)S(1)}, u32[]{:S(2)}) copy-start(f32[256,256]{1,0:T(8,128)S(1)} %fusion.36) | copy-start | bytes 786436
  306.8 59.8 %copy-start.2 = (f32[320,320]{1,0:T(8,128)S(1)}, f32[320,320]{1,0:T(8,128)}, u32[]{:S(2)}) copy-start(f32[320,320]{1,0:T(8,128)} %all-reduce.8.cloned.1.call-done) | copy-start | bytes 1228804
  470.6 2.9 copy-start.6
  470.6 2.9 copy-start.7
  475.8 80.2 %all-reduce.12.cloned.1.call-start = ((), (), s32[]{:S(2)}) async-start(), calls=%async_computation.3 | async-start | bytes 196608 | tf_op jit(solution)/shard_map/psum | solution.py:21
  509.4 80.9 %all-reduce.14.cloned.1.call-start = ((), (), s32[]{:S(2)}) async-start(), calls=%async_computation.4 | async-start | bytes 196608 | tf_op jit(solution)/shard_map/psum | solution.py:21
  556.0 69.7 %all-reduce.16.cloned.1.call-start = ((), (), s32[]{:S(2)}) async-start(), calls=%async_computation.5 | async-start | bytes 196608 | tf_op jit(solution)/shard_map/psum | solution.py:21
  590.3 106.5 %all-reduce.18.cloned.1.call-start = ((), (), s32[]{:S(2)}) async-start(), calls=%async_computation.6 | async-start | bytes 196608 | tf_op jit(solution)/shard_map/psum | solution.py:21
  763.8 60.4 %copy-start.4 = (f32[256,256]{1,0:T(8,128)S(1)}, f32[256,256]{1,0:T(8,128)}, u32[]{:S(2)}) copy-start(f32[256,256]{1,0:T(8,128)} %copy-done.3) | copy-start | bytes 786436
  876.4 11.7 %copy-start.1 = (f32[256,1024]{1,0:T(8,128)}, f32[256,1024]{1,0:T(8,128)S(1)}, u32[]{:S(2)}) copy-start(f32[256,1024]{1,0:T(8,128)S(1)} %fusion.6) | copy-start | bytes 3145732
  876.4 9.6 %copy-start.8 = (f32[64,256]{0,1:T(8,128)S(1)}, f32[64,256]{0,1:T(8,128)}, u32[]{:S(2)}) copy-start(f32[64,256]{0,1:T(8,128)} %fusion.85) | copy-start | bytes 196612
Sparse Core Ops, SparseCore 0:
  50.5 253.9 all-reduce.7
  475.9 33.4 all-reduce.9
  511.7 44.2 all-reduce.11
  558.4 31.8 all-reduce.13
  592.7 33.0 all-reduce.15
  627.9 68.8 all-reduce.17
where the time goes:
time: 906 us; the launch traced here: 895 us
  waiting for transfers between devices  484 us (53%)
  other arithmetic  304 us (34%)
  local copies, waits for them, and re-layouts  35.8 us (4%)
  matrix products  35.3 us (4%)
  between operations  24.8 us (3%)
  starting transfers between devices  10.6 us (1%)
    psum x1, waiting for transfers between devices, local(): gram_one = lax.psum(product(stacked, stacked.T), GRP_SUB)  254 us
    psum x5, waiting for transfers between devices, one_axis_at_a_time(): x = lax.psum(x, axis)  217 us
    another operation x16, other arithmetic, orthonormal(): factor = jnp.linalg.cholesky(symmetric(product(columns.T, columns)))  72.3 us
    another operation x14, other arithmetic, shrink_factors(): inverse_root = lower_inverse(jnp.linalg.cholesky(reduced))  69.7 us
    another operation x14, other arithmetic, shrink_factors(): shrink_factor = jnp.linalg.cholesky(symmetric(keeper)).T  69.3 us
    another operation x7, other arithmetic, orthonormal(): return jax.scipy.linalg.solve_triangular(factor, columns.T, lower=True).T  43.2 us
    another operation x6, other arithmetic, lower_inverse(): return jax.scipy.linalg.solve_triangular(triangle, identity, lower=True)  42.5 us
    dot_general x28, matrix products, product(): jnp.dot(former, latter, precision=highest, preferred_element_type=jnp.flo...  28 us
  transfers between devices with their start and end apart: 7, of which 7 were waited for; matrix products, arithmetic and copies ran while one was open for 0% of the time, Pallas kernels for 0%

commit v1 on v0

v1 whole, which is shorter than its diff:
```python
import jax
import jax.numpy as jnp
from jax import lax
from jax.experimental import pallas as pl
from jax.experimental.pallas import tpu as pltpu
from jax.sharding import Mesh
from jax.sharding import PartitionSpec as P

SUB = ("sub_0", "sub_1")
GRP_SUB = ("grp_0", "grp_1", "grp_2", "sub_0", "sub_1")
GRP = ("grp_0", "grp_1", "grp_2")

F32 = jnp.float32
HI = lax.Precision.HIGHEST
BLK = 32


def nn(a, b):
    return lax.dot_general(a, b, (((1,), (0,)), ((), ())), precision=HI, preferred_element_type=F32)


def nt(a, b):
    return lax.dot_general(a, b, (((1,), (1,)), ((), ())), precision=HI, preferred_element_type=F32)


def tn(a, b):
    return lax.dot_general(a, b, (((0,), (0,)), ((), ())), precision=HI, preferred_element_type=F32)


def iota(shape, axis):
    return lax.broadcasted_iota(jnp.int32, shape, axis)


def spread(tile, row):
    return jnp.broadcast_to(tile[row : row + 1], (8, 128))


def pivot_block(block, rows):
    groups = BLK // 8
    cols = []
    for j in range(BLK):
        cols.append([jnp.broadcast_to(block[8 * t : 8 * t + 8, j : j + 1], (8, 128)) if t >= j // 8 else None for t in range(groups)])
    sub = iota((8, 128), 0)
    width = len(rows[0])
    pivots = [None] * groups
    for k in range(BLK):
        tk, sk = divmod(k, 8)
        pivot = spread(cols[k][tk], sk)
        inverse = 1.0 / pivot
        scaled = [None] * groups
        for t in range(tk, groups):
            scaled[t] = cols[k][t] * inverse
        scaled[tk] = jnp.where(sub > sk, scaled[tk], 0.0)
        for j in range(k + 1, BLK):
            tj, sj = divmod(j, 8)
            element = spread(cols[k][tj], sj)
            for t in range(tj, groups):
                cols[j][t] = cols[j][t] - scaled[t] * element
        for c in range(width):
            row = spread(rows[tk][c], sk)
            for t in range(tk, groups):
                rows[t][c] = rows[t][c] - scaled[t] * row
        pivots[tk] = pivot if sk == 0 else jnp.where(sub == sk, pivot, pivots[tk])
    for t in range(groups):
        root = lax.rsqrt(pivots[t])
        for c in range(width):
            rows[t][c] = rows[t][c] * root
    return rows


def factor(work, width):
    tiles = width // 128

    def step(p, _):
        base = pl.multiple_of(p * BLK, BLK)
        lane = pl.multiple_of((p // 4) * 128, 128)
        block = work[pl.ds(base, BLK), pl.ds(lane, 128)]
        block = pltpu.roll(block, lax.rem(128 - (p % 4) * BLK, 128), 1)
        rows = [[work[pl.ds(base + 8 * t, 8), c * 128 : c * 128 + 128] for c in range(tiles)] for t in range(BLK // 8)]
        rows = pivot_block(block, rows)
        for t in range(BLK // 8):
            for c in range(tiles):
                work[pl.ds(base + 8 * t, 8), c * 128 : c * 128 + 128] = rows[t][c]

        panel = jnp.concatenate([jnp.concatenate(r, axis=1) for r in rows], axis=0)
        left = jnp.where(iota((BLK, 256), 1) >= base + BLK, panel[:, :256], 0.0)

        @pl.when(p < 3)
        def _():
            work[0:128, 0:width] = work[0:128, 0:width] - tn(left[:, :128], panel)

        @pl.when(p < 7)
        def _():
            work[128:256, 0:width] = work[128:256, 0:width] - tn(left[:, 128:], panel)
        return 0

    lax.fori_loop(0, 256 // BLK, step, 0)


def sym(x):
    return 0.5 * (x + x.T)


def shrink(yt, gram, work, yt_width):
    eye = (iota((256, 256), 0) == iota((256, 256), 1)).astype(F32)
    upper = iota((256, 256), 0) <= iota((256, 256), 1)
    work[:, 0:256] = nt(yt, yt)
    work[:, 256:640] = yt
    factor(work, 640)
    qt = work[:, 256:640]
    reduced = sym(nt(nn(qt, gram), qt))
    work[:, 0:256] = reduced
    work[:, 256:512] = eye
    factor(work, 512)
    root = work[:, 256:512]
    offset = 0.5 / jnp.sum(root * root, keepdims=True)
    work[:, 0:256] = eye - offset * tn(root, root)
    factor(work, 256)
    keeper = jnp.where(upper, work[:, 0:256], 0.0)
    return nn(keeper, qt), keeper, reduced


def small(matrix, right):
    tiles = right.shape[1] // 128
    rows = [[right[8 * t : 8 * t + 8, c * 128 : c * 128 + 128] for c in range(tiles)] for t in range(BLK // 8)]
    rows = pivot_block(matrix, rows)
    return jnp.concatenate([jnp.concatenate(r, axis=1) for r in rows], axis=0)


def chain_kernel(gram_ref, coef_ref, work, second_gram):
    lanes = iota((256, 384), 1)
    yt = jnp.where(lanes < 320, gram_ref[0:256, :], 0.0)
    inner = (iota((384, 384), 0) < 320) & (iota((384, 384), 1) < 320)
    second_gram[...] = jnp.where(inner, gram_ref[...], 0.0)
    weights, keeper, reduced = shrink(yt, second_gram[...], work, 640)
    corner = sym(nt(nn(keeper, reduced), keeper))
    mixed = nn(weights, gram_ref[...])
    side = mixed[:, 256:384]
    tail = gram_ref[256:384, 256:384]
    side = jnp.where(iota((256, 128), 1) < 64, pltpu.roll(side, 64, 1), 0.0)
    tail = pltpu.roll(tail, 64, 1)[64:128]
    tail = jnp.where(iota((64, 128), 1) < 64, tail, 0.0)
    second_gram[0:256, 0:256] = corner
    second_gram[0:256, 256:384] = side
    second_gram[256:384, 0:256] = side.T
    second_gram[256:320, 256:384] = tail
    second_gram[320:384, 256:384] = jnp.zeros((64, 128), F32)
    weights_two, keeper_two, reduced_two = shrink(second_gram[0:256, :], second_gram[...], work, 640)
    shifted = jnp.where(iota((256, 128), 1) >= 64, pltpu.roll(weights_two[:, 256:384], 64, 1), 0.0)
    whole = nn(weights_two[:, :256], weights)
    whole = jnp.concatenate([whole[:, :256], whole[:, 256:] + shifted], axis=1)
    coef_ref[0:256, :] = whole
    spectrum = sym(nt(nn(keeper_two, reduced_two), keeper_two))
    leading = spectrum[0:32, :]
    block = nt(leading, jnp.concatenate([leading, jnp.zeros((96, 256), F32)], axis=0))
    ut = small(block, leading)
    padded = jnp.concatenate([ut, jnp.zeros((96, 256), F32)], axis=0)
    block = nt(nn(ut, spectrum), padded)
    block = 0.5 * (block + nt(ut, jnp.concatenate([nn(ut, spectrum), jnp.zeros((96, 256), F32)], axis=0)))
    towards = nn(ut, whole)
    scores = nn(towards, gram_ref[...])[:, 256:384]
    both = small(block, jnp.concatenate([towards, scores], axis=1))
    ident = (iota((128, 384), 1) == iota((128, 384), 0) + 256).astype(F32)
    coef_ref[256:384, :] = ident - tn(both[:, 384:512], both[:, :384])


def chain(gram):
    return pl.pallas_call(
        chain_kernel,
        out_shape=jax.ShapeDtypeStruct((384, 384), F32),
        in_specs=[pl.BlockSpec(memory_space=pltpu.VMEM)],
        out_specs=pl.BlockSpec(memory_space=pltpu.VMEM),
        scratch_shapes=[pltpu.VMEM((256, 640), F32), pltpu.VMEM((384, 384), F32)],
    )(gram)


def local(arrivals, sketch, owner, slot):
    arrived_rows, arrived_columns = arrivals.shape
    host_count = owner.shape[0]
    shaped = arrivals.reshape(arrived_rows, host_count, arrived_columns // host_count)
    placed = jnp.take(shaped, owner, axis=1).reshape(arrived_rows, arrived_columns)
    regrouped = lax.all_to_all(placed, SUB, split_axis=1, concat_axis=0, tiled=True)
    samples = jnp.take(regrouped, slot, axis=0)
    stacked = jnp.concatenate([sketch, samples], axis=0)
    gram = lax.psum(nt(stacked, stacked), GRP_SUB)
    outs = nn(chain(gram), stacked)
    return (outs[:256], outs[256:])


def solution(mesh):
    split = Mesh(mesh.devices.reshape(2, 4, 2, 2, 8), ("grp_0", "grp_1", "grp_2", "sub_0", "sub_1"))
    placed = (P(SUB, GRP), P(None, GRP_SUB), P(GRP), P())
    return jax.shard_map(
        local,
        mesh=split,
        in_specs=placed,
        out_specs=(P(None, GRP_SUB), P(None, GRP_SUB)),
        check_vma=False,
    )
```

time: 906 us -> 390 us (0.43); the launches traced: 895 us -> 390 us
  other arithmetic: 304 us -> 1.55 us
  waiting for transfers between devices: 484 us -> 267 us
  Pallas kernels: 0 us -> 73.6 us
  matrix products: 35.3 us -> 7.23 us
  local copies, waits for them, and re-layouts: 35.8 us -> 15.6 us
  between operations: 24.8 us -> 14.1 us
    another operation x60 -> x0, other arithmetic: 301 us -> none  [the longest x16 72.3 us: orthonormal(): factor = jnp.linalg.cholesky(symmetric(product(columns.T, columns)))]
    psum x6 -> x1, waiting for transfers between devices: 471 us -> 254 us  [local(): gram = lax.psum(nt(stacked, stacked), GRP_SUB)]
    pallas_call x0 -> x1, Pallas kernels: none -> 73.6 us  [chain(): pl.pallas_call(chain_kernel, out_shape=jax.ShapeDtypeStruct((384, 384), F...]
    dot_general x28 -> x2, matrix products: 28 us -> 7.23 us  [the longest x1 3.73 us: nn(): lax.dot_general(a, b, (((1,), (0,)), ((), ())), precision=HI, preferred_e...]
    another operation x41 -> x0, local copies, waits for them, and re-layouts: 16.1 us -> none  [the longest x12 7.97 us: lower_inverse(): return jax.scipy.linalg.solve_triangular(triangle, identity, lower=True)]
  transfers between devices with their start and end apart: 7 -> 2, of which waited for: 7 -> 2; matrix products, arithmetic and copies ran while one was open for 0% -> 0% of each run, Pallas kernels for 0% -> 0%
where the time goes in v1:
time: 390 us
  waiting for transfers between devices  267 us (68%)
  Pallas kernels  73.6 us (19%)
  local copies, waits for them, and re-layouts  15.6 us (4%)
  between operations  14.1 us (4%)
  starting transfers between devices  10.2 us (3%)
  matrix products  7.23 us (2%)
    psum x1, waiting for transfers between devices, local(): gram = lax.psum(nt(stacked, stacked), GRP_SUB)  254 us
    pallas_call x1, Pallas kernels, chain(): pl.pallas_call(chain_kernel, out_shape=jax.ShapeDtypeStruct((384, 384), F...  73.6 us
    all_to_all x1, waiting for transfers between devices, local(): lax.all_to_all(placed, SUB, split_axis=1, concat_axis=0, tiled=True)  13.7 us
    all_to_all x1, starting transfers between devices, local(): lax.all_to_all(placed, SUB, split_axis=1, concat_axis=0, tiled=True)  10.1 us
  transfers between devices with their start and end apart: 2, of which 2 were waited for; matrix products, arithmetic and copies ran while one was open for 0% of the time, Pallas kernels for 0%

profile of v1, /device:TPU:1, one launch (start us, length us, event | category | flops | bytes accessed | tf_op | source)
XLA Modules:
  0.0 389.5 jit_solution(6044869282888976144)
XLA Ops:
  7.2 0.7 compare_select_fusion
  7.8 0.7 compare_and_fusion
  8.5 1.7 reshape.31
  10.3 2.5 copy.9
  12.8 3.9 gather_fusion
  16.7 2.0 copy.10
  18.7 1.0 gather.11
  19.6 0.1 broadcast_in_dim.31
  19.7 0.1 broadcast_in_dim.32
  19.9 0.2 broadcast_in_dim.33
  20.0 0.0 copy-start.1
  20.1 1.1 copy.11
  21.2 10.1 %all-to-all-start = ((f32[8,16,1024]{2,0,1:T(8,128)}), f32[8,16,1024]{2,0,1:T(8,128)S(1)}, u32[]{:S(2)}, u32[]{:S(2)}) async-start(f32[8,16,1024]{2,0,1:T(8,128)} %copy.11), calls=%async_computation | async-start | bytes 1048576 | tf_op jit(solution)/shard_map/all_to_all | solution.py:182
  31.3 0.0 all-reduce.2.cloned.1.call-start
  31.4 0.0 copy-done.1
  31.4 13.7 %all-to-all-done = f32[8,16,1024]{2,0,1:T(8,128)S(1)} async-done(((f32[8,16,1024]{2,0,1:T(8,128)}), f32[8,16,1024]{2,0,1:T(8,128)S(1)}, u32[]{:S(2)}, u32[]{:S(2)}) %all-to-all-start) | async-done | bytes 524320 | tf_op jit(solution)/shard_map/all_to_all | solution.py:182
  45.1 0.0 copy-start
  45.1 0.8 gather_fusion.1
  45.9 0.1 broadcast_select_fusion
  46.1 0.3 copy-done
  46.4 3.5 fusion.1
  49.9 0.0 all-reduce.2.cloned.1.call-update
  49.9 253.5 %all-reduce.2.cloned.1.call-done.gram_ref = f32[384,384]{1,0:T(8,128)} async-done(((f32[384,384]{1,0:T(8,128)}), f32[384,384]{1,0:T(8,128)}) %all-reduce.2.cloned.1.call-update) | async-done | bytes 589840 | tf_op jit(solution)/shard_map/psum | solution.py:185
  303.4 73.6 %shard_map.59 = f32[384,384]{1,0:T(8,128)} custom-call(f32[384,384]{1,0:T(8,128)} %all-reduce.2.cloned.1.call-done.gram_ref), custom_call_target="tpu_custom_call" | custom-call | tf_op jit(solution)/shard_map/pallas_call | solution.py:168
  377.0 3.7 fusion
  380.8 1.1 slice.12
  381.9 0.8 slice.13
  (5 shorter events, 0.1 us)
Async XLA Ops:
  20.0 11.3 %copy-start.1 = (s32[128]{0:T(128)S(1)}, s32[128]{0:T(128)}, u32[]{:S(2)}) copy-start(s32[128]{0:T(128)} %param.7) | copy-start | bytes 1540
  21.2 23.9 %all-to-all-start = ((f32[8,16,1024]{2,0,1:T(8,128)}), f32[8,16,1024]{2,0,1:T(8,128)S(1)}, u32[]{:S(2)}, u32[]{:S(2)}) async-start(f32[8,16,1024]{2,0,1:T(8,128)} %copy.11), calls=%async_computation | async-start | bytes 1048576 | tf_op jit(solution)/shard_map/all_to_all | solution.py:182
  31.3 272.1 %all-reduce.2.cloned.1.call-start = ((), (), s32[]{:S(2)}) async-start(), calls=%async_computation.1 | async-start | bytes 1179648 | tf_op jit(solution)/shard_map/psum | solution.py:185
  45.1 1.2 copy-start
Sparse Core Ops, SparseCore 0:
  50.0 253.3 all-reduce.1

commit v2 on v1

--- a/solution.py
+++ b/solution.py
@@ -127,7 +127,15 @@
     return jnp.concatenate([jnp.concatenate(r, axis=1) for r in rows], axis=0)
 
 
-def chain_kernel(gram_ref, coef_ref, work, second_gram):
+def chain_kernel(packed_ref, sketch_ref, samples_ref, final_ref, residual_ref, work, gram_ref, second_gram, coef_ref):
+    index = 0
+    for i in range(3):
+        for j in range(i + 1):
+            tile = packed_ref[index * 128 : index * 128 + 128, :]
+            gram_ref[i * 128 : i * 128 + 128, j * 128 : j * 128 + 128] = tile
+            if i != j:
+                gram_ref[j * 128 : j * 128 + 128, i * 128 : i * 128 + 128] = tile.T
+            index += 1
     lanes = iota((256, 384), 1)
     yt = jnp.where(lanes < 320, gram_ref[0:256, :], 0.0)
     inner = (iota((384, 384), 0) < 320) & (iota((384, 384), 1) < 320)
@@ -164,27 +172,211 @@
     coef_ref[256:384, :] = ident - tn(both[:, 384:512], both[:, :384])
 
 
-def chain(gram):
+    def columns(i, _):
+        at = pl.ds(pl.multiple_of(i * 256, 256), 256)
+        both = nn(coef_ref[:, 0:256], sketch_ref[:, at]) + nn(coef_ref[:, 256:384], samples_ref[:, at])
+        final_ref[:, at] = both[:256]
+        residual_ref[:, at] = both[256:]
+        return 0
+
+    lax.fori_loop(0, 4, columns, 0)
+
+
+def chain(packed, sketch, samples):
+    vmem = pl.BlockSpec(memory_space=pltpu.VMEM)
     return pl.pallas_call(
         chain_kernel,
-        out_shape=jax.ShapeDtypeStruct((384, 384), F32),
+        out_shape=(jax.ShapeDtypeStruct((256, 1024), F32), jax.ShapeDtypeStruct((128, 1024), F32)),
+        in_specs=[vmem] * 3,
+        out_specs=(vmem, vmem),
+        scratch_shapes=[pltpu.VMEM((256, 640), F32), pltpu.VMEM((384, 384), F32), pltpu.VMEM((384, 384), F32), pltpu.VMEM((384, 384), F32)],
+    )(packed, sketch, samples)
+
+
+def gram_kernel(slot_ref, sketch_ref, landed_ref, packed_ref, samples_ref):
+    pick = (iota((128, 128), 0) == slot_ref[...]).astype(F32)
+    samples_ref[...] = tn(pick, landed_ref[...])
+    packed_ref[0:128, :] = nt(sketch_ref[0:128, :], sketch_ref[0:128, :])
+    packed_ref[128:256, :] = nt(sketch_ref[128:256, :], sketch_ref[0:128, :])
+    packed_ref[256:384, :] = nt(sketch_ref[128:256, :], sketch_ref[128:256, :])
+    packed_ref[384:512, :] = nt(samples_ref[...], sketch_ref[0:128, :])
+    packed_ref[512:640, :] = nt(samples_ref[...], sketch_ref[128:256, :])
+    packed_ref[640:768, :] = nt(samples_ref[...], samples_ref[...])
+
+
+def gram_terms(slot, sketch, landed):
+    vmem = pl.BlockSpec(memory_space=pltpu.VMEM)
+    return pl.pallas_call(
+        gram_kernel,
+        out_shape=(jax.ShapeDtypeStruct((768, 128), F32), jax.ShapeDtypeStruct((128, 1024), F32)),
+        in_specs=[vmem] * 3,
+        out_specs=(vmem, vmem),
+    )(slot, sketch, landed)
+
+
+def place_kernel(owner_ref, arrivals_ref, out_ref):
+    quarter = lax.broadcasted_iota(jnp.int32, (8, 128), 1) // 32
+
+    def step(v, _):
+        pieces = []
+        for i in range(4):
+            host = owner_ref[v * 4 + i]
+            tile = arrivals_ref[:, pl.ds(pl.multiple_of((host // 4) * 128, 128), 128)]
+            pieces.append(pltpu.roll(tile, lax.rem(i * 32 - lax.rem(host, 4) * 32 + 128, 128), 1))
+        tile = jnp.where(quarter == 0, pieces[0], jnp.where(quarter == 1, pieces[1], jnp.where(quarter == 2, pieces[2], pieces[3])))
+        out_ref[v // 8, :, pl.ds(pl.multiple_of(lax.rem(v, 8) * 128, 128), 128)] = tile
+        return 0
+
+    lax.fori_loop(0, 128, step, 0, unroll=16)
+
+
+def place(owner, arrivals):
+    return pl.pallas_call(
+        place_kernel,
+        out_shape=jax.ShapeDtypeStruct((16, 8, 1024), F32),
+        in_specs=[pl.BlockSpec(memory_space=pltpu.SMEM), pl.BlockSpec(memory_space=pltpu.VMEM)],
+        out_specs=pl.BlockSpec(memory_space=pltpu.VMEM),
+    )(owner, arrivals)
+
+
+MESH = pl.DeviceIdType.MESH
+
+
+def spot():
+    return tuple(lax.axis_index(name) for name in GRP_SUB)
+
+
+def exchange_kernel(placed_ref, out_ref, landed, send_sems, recv_sems, own_sem):
+    y_hi, x, core, y_lo, z = spot()
+    me = y_lo * 8 + z
+
+    def device(j):
+        return (y_hi, x, core, j // 8, lax.rem(j, 8))
+
+    barrier = pltpu.get_barrier_semaphore()
+    for s in range(1, 16):
+        pl.semaphore_signal(barrier, inc=1, device_id=device(lax.rem(me + s, 16)), device_id_type=MESH)
+    own = pltpu.make_async_copy(placed_ref.at[me], landed.at[me], own_sem)
+    own.start()
+    pl.semaphore_wait(barrier, 15)
+    copies = []
+    for s in (8, 4, 12, 3, 5, 11, 13, 2, 6, 10, 14, 1, 7, 9, 15):
+        peer = lax.rem(me + s, 16)
+        copy = pltpu.make_async_remote_copy(
+            src_ref=placed_ref.at[peer], dst_ref=landed.at[me],
+            send_sem=send_sems.at[s], recv_sem=recv_sems.at[s],
+            device_id=device(peer), device_id_type=MESH)
+        copy.start()
+        copies.append(copy)
+    own.wait()
+    for copy in copies:
+        copy.wait_recv()
+    out_ref[...] = landed[...]
+    for copy in copies:
+        copy.wait_send()
+
+
+def exchange(placed):
+    return pl.pallas_call(
+        exchange_kernel,
+        out_shape=jax.ShapeDtypeStruct((16, 8, 1024), F32),
         in_specs=[pl.BlockSpec(memory_space=pltpu.VMEM)],
         out_specs=pl.BlockSpec(memory_space=pltpu.VMEM),
-        scratch_shapes=[pltpu.VMEM((256, 640), F32), pltpu.VMEM((384, 384), F32)],
-    )(gram)
+        scratch_shapes=[pltpu.VMEM((16, 8, 1024), F32), pltpu.SemaphoreType.DMA((16,)), pltpu.SemaphoreType.DMA((16,)), pltpu.SemaphoreType.DMA],
+        compiler_params=pltpu.CompilerParams(collective_id=0, has_side_effects=True),
+    )(placed)
+
+
+def reduce_kernel(part_ref, out_ref, twin, half, plane, piece, column, share, whole,
+                  twin_sems, plane_send, plane_recv, column_send, column_recv, share_send, share_recv, back_send, back_recv):
+    y_hi, x, core, y_lo, z = spot()
+    me = (y_hi * 2 + y_lo) * 4 + x
+
+    def in_plane(q):
+        y = q // 4
+        return (y // 2, lax.rem(q, 4), core, lax.rem(y, 2), z)
+
+    def in_column(k):
+        return (y_hi, x, core, y_lo, k)
+
+    other = (y_hi, x, 1 - core, y_lo, z)
+    barrier = pltpu.get_barrier_semaphore()
+    pl.semaphore_signal(barrier, inc=1, device_id=other, device_id_type=MESH)
+    for s in range(1, 16):
+        pl.semaphore_signal(barrier, inc=1, device_id=in_plane(lax.rem(me + s, 16)), device_id_type=MESH)
+    for s in range(1, 8):
+        pl.semaphore_signal(barrier, inc=1, device_id=in_column(lax.rem(z + s, 8)), device_id_type=MESH)
+    pl.semaphore_wait(barrier, 23)
+
+    def send(source, target, send_sem, recv_sem, device):
+        copy = pltpu.make_async_remote_copy(src_ref=source, dst_ref=target, send_sem=send_sem, recv_sem=recv_sem, device_id=device, device_id_type=MESH)
+        copy.start()
+        return copy
+
+    first = send(part_ref.at[1 - core], twin, twin_sems.at[0], twin_sems.at[1], other)
+    first.wait_recv()
+    half[...] = part_ref[core] + twin[...]
+
+    scattered = []
+    for s in range(1, 16):
+        peer = lax.rem(me + s, 16)
+        scattered.append(send(half.at[peer], plane.at[s], plane_send.at[s], plane_recv.at[s], in_plane(peer)))
+    total = half[me]
+    for s in range(1, 16):
+        scattered[s - 1].wait_recv()
+        total = total + plane[s]
+    piece[...] = total
+
+    spread_out = []
+    for s in range(1, 8):
+        peer = lax.rem(z + s, 8)
+        spread_out.append(send(piece, column.at[z], column_send.at[s], column_recv.at[s], in_column(peer)))
+    column[z] = piece[...]
+    for copy in spread_out:
+        copy.wait_recv()
+    total = column[0]
+    for k in range(1, 8):
+        total = total + column[k]
+    share[...] = total
+
+    gathered = []
+    for s in range(1, 16):
+        peer = lax.rem(me + s, 16)
+        gathered.append(send(share, whole.at[core, me], share_send.at[s], share_recv.at[s], in_plane(peer)))
+    whole[core, me] = share[...]
+    back = [send(share, whole.at[core, me], back_send.at[0], back_recv.at[0], other)]
+    for s in range(1, 16):
+        gathered[s - 1].wait_recv()
+        source = lax.rem(me + 16 - s, 16)
+        back.append(send(whole.at[core, source], whole.at[core, source], back_send.at[s], back_recv.at[s], other))
+    for copy in back:
+        copy.wait_recv()
+    out_ref[...] = whole[...]
+    for copy in [first] + scattered + spread_out + gathered + back:
+        copy.wait_send()
+
+
+def reduce_all(part):
+    dma = pltpu.SemaphoreType.DMA
+    return pl.pallas_call(
+        reduce_kernel,
+        out_shape=jax.ShapeDtypeStruct((2, 16, 24, 128), F32),
+        in_specs=[pl.BlockSpec(memory_space=pltpu.VMEM)],
+        out_specs=pl.BlockSpec(memory_space=pltpu.VMEM),
+        scratch_shapes=[
+            pltpu.VMEM((16, 24, 128), F32), pltpu.VMEM((16, 24, 128), F32), pltpu.VMEM((16, 24, 128), F32),
+            pltpu.VMEM((24, 128), F32), pltpu.VMEM((8, 24, 128), F32), pltpu.VMEM((24, 128), F32), pltpu.VMEM((2, 16, 24, 128), F32),
+            dma((2,)), dma((16,)), dma((16,)), dma((8,)), dma((8,)), dma((16,)), dma((16,)), dma((16,)), dma((16,)),
+        ],
+        compiler_params=pltpu.CompilerParams(collective_id=1, has_side_effects=True),
+    )(part)
 
 
 def local(arrivals, sketch, owner, slot):
-    arrived_rows, arrived_columns = arrivals.shape
-    host_count = owner.shape[0]
-    shaped = arrivals.reshape(arrived_rows, host_count, arrived_columns // host_count)
-    placed = jnp.take(shaped, owner, axis=1).reshape(arrived_rows, arrived_columns)
-    regrouped = lax.all_to_all(placed, SUB, split_axis=1, concat_axis=0, tiled=True)
-    samples = jnp.take(regrouped, slot, axis=0)
-    stacked = jnp.concatenate([sketch, samples], axis=0)
-    gram = lax.psum(nt(stacked, stacked), GRP_SUB)
-    outs = nn(chain(gram), stacked)
-    return (outs[:256], outs[256:])
+    landed = exchange(place(owner, arrivals)).reshape(128, 1024)
+    packed, samples = gram_terms(slot.reshape(1, 128), sketch, landed)
+    total = reduce_all(packed.reshape(2, 16, 24, 128)).reshape(768, 128)
+    return chain(total, sketch, samples)
 
 
 def solution(mesh):

time: 390 us -> 142 us (0.36)
  waiting for transfers between devices: 267 us -> 0 us
  Pallas kernels: 73.6 us -> 141 us
  local copies, waits for them, and re-layouts: 15.6 us -> 0 us
  between operations: 14.1 us -> 0.65 us
  starting transfers between devices: 10.2 us -> 0 us
  matrix products: 7.23 us -> 0 us
    psum x1 -> x0, waiting for transfers between devices: 254 us -> none  [local(): gram = lax.psum(nt(stacked, stacked), GRP_SUB)]
    pallas_call x1 -> x5, Pallas kernels: 73.6 us -> 141 us  [the longest x1 77.2 us: chain(): pl.pallas_call(chain_kernel, out_shape=(jax.ShapeDtypeStruct((256, 1024),...]
    all_to_all x1 -> x0, waiting for transfers between devices: 13.7 us -> none  [local(): lax.all_to_all(placed, SUB, split_axis=1, concat_axis=0, tiled=True)]
    all_to_all x1 -> x0, starting transfers between devices: 10.1 us -> none  [local(): lax.all_to_all(placed, SUB, split_axis=1, concat_axis=0, tiled=True)]
    gather x4 -> x0, local copies, waits for them, and re-layouts: 7.61 us -> none  [the longest x3 6.82 us: local(): jnp.take(shaped, owner, axis=1).reshape(arrived_rows, arrived_columns)]
    dot_general x2 -> x0, matrix products: 7.23 us -> none  [the longest x1 3.73 us: nn(): lax.dot_general(a, b, (((1,), (0,)), ((), ())), precision=HI, preferred_e...]
    reshape x2 -> x0, local copies, waits for them, and re-layouts: 4.27 us -> none  [local(): arrivals.reshape(arrived_rows, host_count, arrived_columns // host_count)]
  transfers between devices with their start and end apart: 2 -> 0, of which waited for: 2 -> 0; matrix products, arithmetic and copies ran while one was open for 0% -> 0% of each run, Pallas kernels for 0% -> 0%
where the time goes in v2:
time: 142 us
  Pallas kernels  141 us (99%)
    pallas_call x1, Pallas kernels, chain(): pl.pallas_call(chain_kernel, out_shape=(jax.ShapeDtypeStruct((256, 1024),...  77.2 us
    pallas_call x1, Pallas kernels, reduce_all(): pl.pallas_call(reduce_kernel, out_shape=jax.ShapeDtypeStruct((2, 16, 24,...  28.5 us
    pallas_call x1, Pallas kernels, exchange(): pl.pallas_call(exchange_kernel, out_shape=jax.ShapeDtypeStruct((16, 8, 10...  23.6 us
    pallas_call x1, Pallas kernels, place(): pl.pallas_call(place_kernel, out_shape=jax.ShapeDtypeStruct((16, 8, 1024)...  6.31 us
    pallas_call x1, Pallas kernels, gram_terms(): pl.pallas_call(gram_kernel, out_shape=(jax.ShapeDtypeStruct((768, 128), F...  5.25 us

profile of v2, /device:TPU:1, one launch (start us, length us, event | category | flops | bytes accessed | tf_op | source)
XLA Modules:
  0.0 141.6 jit_solution(13165279654809167931)
XLA Ops:
  0.6 6.3 %shard_map.59.placed_ref = f32[16,8,1024]{2,1,0:T(8,128)} custom-call(s32[512]{0:T(512)} %owner_ref.1, f32[8,16384]{1,0:T(8,128)} %arrivals_ref.1), custom_call_target="tpu_custom_call" | custom-call | tf_op jit(solution)/shard_map/pallas_call | solution.py:234
  6.9 23.6 %shard_map.60 = f32[16,8,1024]{2,1,0:T(8,128)} custom-call(f32[16,8,1024]{2,1,0:T(8,128)} %shard_map.59.placed_ref), custom_call_target="tpu_custom_call" | custom-call | tf_op jit(solution)/shard_map/pallas_call | solution.py:280
  30.6 5.3 %shard_map.61 = (f32[768,128]{1,0:T(8,128)}, f32[128,1024]{1,0:T(8,128)}) custom-call(s32[1,128]{1,0:T(1,128)} %bitcast.7, f32[256,1024]{1,0:T(8,128)} %sketch_ref.3, f32[128,1024]{1,0:T(8,128)} %bitcast.4), custom_call_target="tpu_custom_call" | custom-call | tf_op jit(solution)/shard_map/pallas_call | solution.py:209
  35.8 28.5 %shard_map.62 = f32[2,16,24,128]{3,2,1,0:T(8,128)} custom-call(f32[2,16,24,128]{3,2,1,0:T(8,128)} %bitcast.6), custom_call_target="tpu_custom_call" | custom-call | tf_op jit(solution)/shard_map/pallas_call | solution.py:361
  64.4 77.2 %shard_map.63 = (f32[256,1024]{1,0:T(8,128)}, f32[128,1024]{1,0:T(8,128)}) custom-call(f32[768,128]{1,0:T(8,128)} %bitcast.5, f32[256,1024]{1,0:T(8,128)} %sketch_ref.3, f32[128,1024]{1,0:T(8,128)} %get-tuple-element.5.samples_ref), custom_call_target="tpu_custom_call" | custom-call | tf_op jit(solution)/shard_map/pallas_call | solution.py:187

commit v3 on v2

v3 whole, which is shorter than its diff:
```python
import jax
import jax.numpy as jnp
from jax import lax
from jax.experimental import pallas as pl
from jax.experimental.pallas import tpu as pltpu
from jax.sharding import Mesh
from jax.sharding import PartitionSpec as P

SUB = ("sub_0", "sub_1")
GRP_SUB = ("grp_0", "grp_1", "grp_2", "sub_0", "sub_1")
GRP = ("grp_0", "grp_1", "grp_2")
MESH = pl.DeviceIdType.MESH

F32 = jnp.float32
HI = lax.Precision.HIGHEST
BLK = 32


def nn(a, b):
    return lax.dot_general(a, b, (((1,), (0,)), ((), ())), precision=HI, preferred_element_type=F32)


def nt(a, b):
    return lax.dot_general(a, b, (((1,), (1,)), ((), ())), precision=HI, preferred_element_type=F32)


def tn(a, b):
    return lax.dot_general(a, b, (((0,), (0,)), ((), ())), precision=HI, preferred_element_type=F32)


def iota(shape, axis):
    return lax.broadcasted_iota(jnp.int32, shape, axis)


def spread(tile, row):
    return jnp.broadcast_to(tile[row : row + 1], (8, 128))


def pivot_block(cols, rows):
    groups = BLK // 8
    sub = iota((8, 128), 0)
    width = len(rows[0])
    roots = [None] * groups
    pivot = spread(cols[0][0], 0)
    for k in range(BLK):
        tk, sk = divmod(k, 8)
        root = lax.rsqrt(pivot)
        inverse = root * root
        if k + 1 < BLK:
            tj, sj = divmod(k + 1, 8)
            element = spread(cols[k][tj], sj)
            pivot = spread(cols[k + 1][tj], sj) - (element * element) * inverse
        scaled = [None] * groups
        for t in range(tk, groups):
            scaled[t] = cols[k][t] * inverse
        scaled[tk] = jnp.where(sub > sk, scaled[tk], 0.0)
        for j in range(k + 1, BLK):
            tj, sj = divmod(j, 8)
            element = spread(cols[k][tj], sj)
            for t in range(tj, groups):
                cols[j][t] = cols[j][t] - scaled[t] * element
        for c in range(width):
            row = spread(rows[tk][c], sk)
            for t in range(tk, groups):
                rows[t][c] = rows[t][c] - scaled[t] * row
        roots[tk] = root if sk == 0 else jnp.where(sub == sk, root, roots[tk])
    for t in range(groups - 1):
        roots[t] = jnp.minimum(roots[t], roots[t] + roots[groups - 1])
    return [[tile * roots[t] for tile in rows[t]] for t in range(groups)]


def columns_of(tiles, offset):
    cols = []
    for j in range(BLK):
        lane = jnp.full((8, 128), j, jnp.int32) + offset
        cols.append([jnp.take_along_axis(tiles[t], lane, axis=1) if t >= j // 8 else None for t in range(BLK // 8)])
    return cols


def join(rows):
    return jnp.concatenate([jnp.concatenate(r, axis=1) for r in rows], axis=0)


def factor(work, last, turned, early, late):
    groups = BLK // 8

    def step(p, low, first, end):
        base = pl.multiple_of(p * BLK, BLK)
        lane = pl.multiple_of((p // 4) * 128, 128)
        span = slice(first * 128, end * 128)
        block = [work[pl.ds(base + 8 * t, 8), pl.ds(lane, 128)] for t in range(groups)]
        rows = [[work[pl.ds(base + 8 * t, 8), c * 128 : c * 128 + 128] for c in range(first, end)] for t in range(groups)]
        cols = columns_of(block, lax.rem(p, 4) * BLK)
        left = jnp.where(iota((256 - low, 128), 0) >= base + BLK - low, turned[low:, :], 0.0)[:, :BLK]
        work[low:, span] = work[low:, span] - nn(left, last[:, span])
        rows = pivot_block(cols, rows)
        for t in range(groups):
            for c in range(first, end):
                work[pl.ds(base + 8 * t, 8), c * 128 : c * 128 + 128] = rows[t][c - first]
        panel = join(rows)
        last[:, span] = panel
        turned[low:, 0:BLK] = panel[:, low - first * 128 : 256 - first * 128].T

        @pl.when(p < 7)
        def _():
            below = pl.ds(base + BLK, BLK)
            work[below, span] = work[below, span] - nn(turned[below, 0:BLK], panel)
        return 0

    last[...] = jnp.zeros_like(last)
    turned[...] = jnp.zeros_like(turned)
    lax.fori_loop(0, 4, lambda p, _: step(p, 0, *early), 0)
    lax.fori_loop(4, 8, lambda p, _: step(p, 128, *late), 0)


def near_identity_root(excess):
    down, across = iota((256, 256), 0), iota((256, 256), 1)
    half = jnp.where(down > across, 1.0, jnp.where(down == across, 0.5, 0.0)).astype(F32)

    def onward(x):
        return -half * (excess + nt(x, x))

    def more(state):
        return (state[1] > 1e-11) & (state[2] < 64)

    def body(state):
        x = onward(state[0])
        y = onward(x)
        return y, jnp.sum((y - x) * (y - x)), state[2] + 1

    return lax.while_loop(more, body, (-half * excess, jnp.float32(1.0), jnp.int32(0)))[0]


def sym(x):
    return 0.5 * (x + x.T)


def shrink(yt, gram, work, last, turned):
    eye = (iota((256, 256), 0) == iota((256, 256), 1)).astype(F32)
    work[:, 0:256] = nt(yt, yt)
    work[:, 256:640] = yt
    factor(work, last, turned, (0, 5), (1, 5))
    qt = work[:, 256:640]
    reduced = sym(nt(nn(qt, gram), qt))
    work[:, 0:256] = reduced
    work[:, 256:512] = eye
    factor(work, last, turned, (0, 3), (1, 4))
    root = work[:, 256:512]
    offset = 0.5 / jnp.sum(root * root, keepdims=True)
    keeper = eye + near_identity_root(offset * tn(root, root)).T
    return nn(keeper, qt), keeper, reduced


def small(matrix, right):
    tiles = right.shape[1] // 128
    groups = BLK // 8
    rows = [[right[8 * t : 8 * t + 8, c * 128 : c * 128 + 128] for c in range(tiles)] for t in range(groups)]
    return join(pivot_block(columns_of([matrix[8 * t : 8 * t + 8] for t in range(groups)], 0), rows))


def chain_kernel(packed_ref, sketch_ref, samples_ref, final_ref, residual_ref, work, last, turned, gram_ref, second_gram, coef_ref):
    index = 0
    for i in range(3):
        for j in range(i + 1):
            tile = packed_ref[index * 128 : index * 128 + 128, :]
            gram_ref[i * 128 : i * 128 + 128, j * 128 : j * 128 + 128] = tile
            if i != j:
                gram_ref[j * 128 : j * 128 + 128, i * 128 : i * 128 + 128] = tile.T
            index += 1
    lanes = iota((256, 384), 1)
    yt = jnp.where(lanes < 320, gram_ref[0:256, :], 0.0)
    inner = (iota((384, 384), 0) < 320) & (iota((384, 384), 1) < 320)
    second_gram[...] = jnp.where(inner, gram_ref[...], 0.0)
    weights, keeper, reduced = shrink(yt, second_gram[...], work, last, turned)
    corner = sym(nt(nn(keeper, reduced), keeper))
    mixed = nn(weights, gram_ref[...])
    side = mixed[:, 256:384]
    tail = gram_ref[256:384, 256:384]
    side = jnp.where(iota((256, 128), 1) < 64, pltpu.roll(side, 64, 1), 0.0)
    tail = pltpu.roll(tail, 64, 1)[64:128]
    tail = jnp.where(iota((64, 128), 1) < 64, tail, 0.0)
    second_gram[0:256, 0:256] = corner
    second_gram[0:256, 256:384] = side
    second_gram[256:384, 0:256] = side.T
    second_gram[256:320, 256:384] = tail
    second_gram[320:384, 256:384] = jnp.zeros((64, 128), F32)
    weights_two, keeper_two, reduced_two = shrink(second_gram[0:256, :], second_gram[...], work, last, turned)
    shifted = jnp.where(iota((256, 128), 1) >= 64, pltpu.roll(weights_two[:, 256:384], 64, 1), 0.0)
    whole = nn(weights_two[:, :256], weights)
    whole = jnp.concatenate([whole[:, :256], whole[:, 256:] + shifted], axis=1)
    coef_ref[0:256, :] = whole
    spectrum = sym(nt(nn(keeper_two, reduced_two), keeper_two))
    leading = spectrum[0:32, :]
    block = nt(leading, jnp.concatenate([leading, jnp.zeros((96, 256), F32)], axis=0))
    ut = small(block, leading)
    padded = jnp.concatenate([ut, jnp.zeros((96, 256), F32)], axis=0)
    block = nt(nn(ut, spectrum), padded)
    block = 0.5 * (block + nt(ut, jnp.concatenate([nn(ut, spectrum), jnp.zeros((96, 256), F32)], axis=0)))
    towards = nn(ut, whole)
    scores = nn(towards, gram_ref[...])[:, 256:384]
    both = small(block, jnp.concatenate([towards, scores], axis=1))
    ident = (iota((128, 384), 1) == iota((128, 384), 0) + 256).astype(F32)
    coef_ref[256:384, :] = ident - tn(both[:, 384:512], both[:, :384])


    def columns(i, _):
        at = pl.ds(pl.multiple_of(i * 256, 256), 256)
        both = nn(coef_ref[:, 0:256], sketch_ref[:, at]) + nn(coef_ref[:, 256:384], samples_ref[:, at])
        final_ref[:, at] = both[:256]
        residual_ref[:, at] = both[256:]
        return 0

    lax.fori_loop(0, 4, columns, 0)


def chain(packed, sketch, samples):
    vmem = pl.BlockSpec(memory_space=pltpu.VMEM)
    square = pltpu.VMEM((384, 384), F32)
    return pl.pallas_call(
        chain_kernel,
        out_shape=(jax.ShapeDtypeStruct((256, 1024), F32), jax.ShapeDtypeStruct((128, 1024), F32)),
        in_specs=[vmem] * 3,
        out_specs=(vmem, vmem),
        scratch_shapes=[pltpu.VMEM((256, 640), F32), pltpu.VMEM((BLK, 640), F32), pltpu.VMEM((256, 128), F32), square, square, square],
    )(packed, sketch, samples)


def spot():
    return tuple(lax.axis_index(name) for name in GRP_SUB)


def place_tile(owner_ref, arrivals_ref, at):
    quarter = iota((8, 128), 1) // 32
    tile = None
    for i in range(4):
        host = owner_ref[at + i]
        source = arrivals_ref[:, pl.ds(pl.multiple_of((host >> 2) * 128, 128), 128)]
        turned = pltpu.roll(source, ((i - host) & 3) * 32, 1)
        tile = turned if i == 0 else jnp.where(quarter == i, turned, tile)
    return tile


def place_kernel(owner_ref, arrivals_ref, placed_ref):
    def block(j, _):
        for v in range(8):
            placed_ref[j, :, v * 128 : v * 128 + 128] = place_tile(owner_ref, arrivals_ref, j * 32 + v * 4)
        return 0

    lax.fori_loop(0, 16, block, 0)


def place(owner, arrivals):
    return pl.pallas_call(
        place_kernel,
        out_shape=jax.ShapeDtypeStruct((16, 8, 1024), F32),
        in_specs=[pl.BlockSpec(memory_space=pltpu.SMEM), pl.BlockSpec(memory_space=pltpu.VMEM)],
        out_specs=pl.BlockSpec(memory_space=pltpu.VMEM),
    )(owner, arrivals)


def collect_kernel(slot_ref, placed, sketch_ref, total_ref, samples_ref,
                   landed, part, twin, half, plane, piece, column, share, whole,
                   move_send, move_recv, twin_sems, plane_send, plane_recv, column_send, column_recv, share_send, share_recv, back_send, back_recv):
    y_hi, x, core, y_lo, z = spot()
    me_sub = y_lo * 8 + z
    me = (y_hi * 2 + y_lo) * 4 + x

    def in_sub(j):
        return (y_hi, x, core, j // 8, lax.rem(j, 8))

    def in_plane(q):
        y = q // 4
        return (y // 2, lax.rem(q, 4), core, lax.rem(y, 2), z)

    def in_column(k):
        return (y_hi, x, core, y_lo, k)

    other = (y_hi, x, 1 - core, y_lo, z)

    def send(source, target, send_sem, recv_sem, device):
        copy = pltpu.make_async_remote_copy(src_ref=source, dst_ref=target, send_sem=send_sem, recv_sem=recv_sem, device_id=device, device_id_type=MESH)
        copy.start()
        return copy

    barrier = pltpu.get_barrier_semaphore()
    pl.semaphore_signal(barrier, inc=1, device_id=other, device_id_type=MESH)
    for s in range(1, 16):
        pl.semaphore_signal(barrier, inc=1, device_id=in_sub(lax.rem(me_sub + s, 16)), device_id_type=MESH)
        pl.semaphore_signal(barrier, inc=1, device_id=in_plane(lax.rem(me + s, 16)), device_id_type=MESH)

    landed[me_sub] = placed[me_sub]
    pl.semaphore_wait(barrier, 31)
    moves = []
    for s in (8, 4, 12, 3, 5, 11, 13, 2, 6, 10, 14, 1, 7, 9, 15):
        peer = lax.rem(me_sub + s, 16)
        moves.append(send(placed.at[peer], landed.at[me_sub], move_send.at[s], move_recv.at[s], in_sub(peer)))

    def put(index, block):
        rows = block.reshape(16, 8, 128)
        for r in range(16):
            at = index * 16 + r
            part[at // 48, (at % 48) // 3, (at % 3) * 8 : (at % 3) * 8 + 8, :] = rows[r]

    put(0, nt(sketch_ref[0:128, :], sketch_ref[0:128, :]))
    put(1, nt(sketch_ref[128:256, :], sketch_ref[0:128, :]))
    put(2, nt(sketch_ref[128:256, :], sketch_ref[128:256, :]))
    for copy in moves:
        copy.wait_recv()
    pick = (iota((128, 128), 0) == slot_ref[...]).astype(F32)
    samples_ref[...] = tn(pick, landed[...].reshape(128, 1024))
    put(3, nt(samples_ref[...], sketch_ref[0:128, :]))
    put(4, nt(samples_ref[...], sketch_ref[128:256, :]))
    put(5, nt(samples_ref[...], samples_ref[...]))

    first = send(part.at[1 - core], twin, twin_sems.at[0], twin_sems.at[1], other)
    first.wait_recv()
    half[...] = part[core] + twin[...]

    scattered = []
    for s in range(1, 16):
        peer = lax.rem(me + s, 16)
        scattered.append(send(half.at[peer], plane.at[s], plane_send.at[s], plane_recv.at[s], in_plane(peer)))
    total = half[me]
    for s in range(1, 16):
        scattered[s - 1].wait_recv()
        total = total + plane[s]
    piece[...] = total

    spread_out = []
    for s in range(1, 8):
        peer = lax.rem(z + s, 8)
        spread_out.append(send(piece, column.at[z], column_send.at[s], column_recv.at[s], in_column(peer)))
    column[z] = piece[...]
    for copy in spread_out:
        copy.wait_recv()
    total = column[0]
    for k in range(1, 8):
        total = total + column[k]
    share[...] = total

    gathered = []
    for s in range(1, 16):
        peer = lax.rem(me + s, 16)
        gathered.append(send(share, whole.at[core, me], share_send.at[s], share_recv.at[s], in_plane(peer)))
    whole[core, me] = share[...]
    back = [send(share, whole.at[core, me], back_send.at[0], back_recv.at[0], other)]
    for s in range(1, 16):
        gathered[s - 1].wait_recv()
        source = lax.rem(me + 16 - s, 16)
        back.append(send(whole.at[core, source], whole.at[core, source], back_send.at[s], back_recv.at[s], other))
    for copy in back:
        copy.wait_recv()
    total_ref[...] = whole[...].reshape(768, 128)
    for copy in moves + [first] + scattered + spread_out + gathered + back:
        copy.wait_send()


def collect(owner, slot, arrivals, sketch):
    dma = pltpu.SemaphoreType.DMA
    vmem = pl.BlockSpec(memory_space=pltpu.VMEM)
    return pl.pallas_call(
        collect_kernel,
        out_shape=(jax.ShapeDtypeStruct((768, 128), F32), jax.ShapeDtypeStruct((128, 1024), F32)),
        in_specs=[vmem, vmem, vmem],
        out_specs=(vmem, vmem),
        scratch_shapes=[
            pltpu.VMEM((16, 8, 1024), F32), pltpu.VMEM((2, 16, 24, 128), F32),
            pltpu.VMEM((16, 24, 128), F32), pltpu.VMEM((16, 24, 128), F32), pltpu.VMEM((16, 24, 128), F32),
            pltpu.VMEM((24, 128), F32), pltpu.VMEM((8, 24, 128), F32), pltpu.VMEM((24, 128), F32), pltpu.VMEM((2, 16, 24, 128), F32),
            dma((16,)), dma((16,)), dma((2,)), dma((16,)), dma((16,)), dma((8,)), dma((8,)), dma((16,)), dma((16,)), dma((16,)), dma((16,)),
        ],
        compiler_params=pltpu.CompilerParams(collective_id=0, has_side_effects=True),
    )(slot, place(owner, arrivals), sketch)


def local(arrivals, sketch, owner, slot):
    packed, samples = collect(owner, slot.reshape(1, 128), arrivals, sketch)
    return chain(packed, sketch, samples)


def solution(mesh):
    split = Mesh(mesh.devices.reshape(2, 4, 2, 2, 8), ("grp_0", "grp_1", "grp_2", "sub_0", "sub_1"))
    placed = (P(SUB, GRP), P(None, GRP_SUB), P(GRP), P())
    return jax.shard_map(
        local,
        mesh=split,
        in_specs=placed,
        out_specs=(P(None, GRP_SUB), P(None, GRP_SUB)),
        check_vma=False,
    )
```

time: 142 us -> 105 us (0.74)
  Pallas kernels: 141 us -> 104 us
    pallas_call x1, Pallas kernels: 77.2 us -> 51 us  [chain(): pl.pallas_call(chain_kernel, out_shape=(jax.ShapeDtypeStruct((256, 1024),...]
    pallas_call x3 -> x1, Pallas kernels: 57.4 us -> 48.6 us  [collect(): pl.pallas_call(collect_kernel, out_shape=(jax.ShapeDtypeStruct((768, 128)...]
    pallas_call x1, Pallas kernels: 6.31 us -> 4.37 us  [place(): pl.pallas_call(place_kernel, out_shape=jax.ShapeDtypeStruct((16, 8, 1024)...]
where the time goes in v3:
time: 105 us
  Pallas kernels  104 us (99%)
    pallas_call x1, Pallas kernels, chain(): pl.pallas_call(chain_kernel, out_shape=(jax.ShapeDtypeStruct((256, 1024),...  51 us
    pallas_call x1, Pallas kernels, collect(): pl.pallas_call(collect_kernel, out_shape=(jax.ShapeDtypeStruct((768, 128)...  48.6 us
    pallas_call x1, Pallas kernels, place(): pl.pallas_call(place_kernel, out_shape=jax.ShapeDtypeStruct((16, 8, 1024)...  4.37 us

profile of v3, /device:TPU:1, one launch (start us, length us, event | category | flops | bytes accessed | tf_op | source)
XLA Modules:
  0.0 104.5 jit_solution(9220866755121553336)
XLA Ops:
  0.6 4.4 %shard_map.59.placed = f32[16,8,1024]{2,1,0:T(8,128)} custom-call(s32[512]{0:T(512)} %owner_ref.1, f32[8,16384]{1,0:T(8,128)} %arrivals_ref.1), custom_call_target="tpu_custom_call" | custom-call | tf_op jit(solution)/shard_map/pallas_call | solution.py:253
  5.0 48.6 %shard_map.60 = (f32[768,128]{1,0:T(8,128)}, f32[128,1024]{1,0:T(8,128)}) custom-call(s32[1,128]{1,0:T(1,128)} %bitcast.1, f32[16,8,1024]{2,1,0:T(8,128)} %shard_map.59.placed, f32[256,1024]{1,0:T(8,128)} %sketch_ref.3), custom_call_target="tpu_custom_call" | custom-call | tf_op jit(solution)/shard_map/pallas_call | solution.py:361
  53.6 51.0 %shard_map.61 = (f32[256,1024]{1,0:T(8,128)}, f32[128,1024]{1,0:T(8,128)}) custom-call(f32[768,128]{1,0:T(8,128)} %get-tuple-element.4.packed_ref, f32[256,1024]{1,0:T(8,128)} %sketch_ref.3, f32[128,1024]{1,0:T(8,128)} %get-tuple-element.5.samples_ref), custom_call_target="tpu_custom_call" | custom-call | tf_op jit(solution)/shard_map/pallas_call | solution.py:219

commit v4 on v3

--- a/solution.py
+++ b/solution.py
@@ -14,6 +14,7 @@
 F32 = jnp.float32
 HI = lax.Precision.HIGHEST
 BLK = 32
+HELD = 16
 
 
 def nn(a, b):
@@ -28,6 +29,20 @@
     return lax.dot_general(a, b, (((0,), (0,)), ((), ())), precision=HI, preferred_element_type=F32)
 
 
+def halves(x):
+    high = x.astype(jnp.bfloat16)
+    return high, (x - high.astype(F32)).astype(jnp.bfloat16)
+
+
+def split_product(a, b, contracted):
+    dims = (((1,), (contracted,)), ((), ()))
+
+    def one(p, q):
+        return lax.dot_general(p, q, dims, preferred_element_type=F32)
+
+    return one(a[0], b[0]) + (one(a[0], b[1]) + one(a[1], b[0]))
+
+
 def iota(shape, axis):
     return lax.broadcasted_iota(jnp.int32, shape, axis)
 
@@ -36,17 +51,22 @@
     return jnp.broadcast_to(tile[row : row + 1], (8, 128))
 
 
-def pivot_block(cols, rows):
+def pivot_block(rows, offset):
     groups = BLK // 8
     sub = iota((8, 128), 0)
     width = len(rows[0])
     roots = [None] * groups
-    pivot = spread(cols[0][0], 0)
+    cols = [None] * BLK
     for k in range(BLK):
         tk, sk = divmod(k, 8)
+        if k % HELD == 0:
+            for j in range(k, k + HELD):
+                lane = jnp.full((8, 128), j, jnp.int32) + offset
+                cols[j] = [jnp.take_along_axis(rows[t][0], lane, axis=1) if t >= j // 8 else None for t in range(groups)]
+            pivot = spread(cols[k][tk], sk)
         root = lax.rsqrt(pivot)
         inverse = root * root
-        if k + 1 < BLK:
+        if (k + 1) % HELD:
             tj, sj = divmod(k + 1, 8)
             element = spread(cols[k][tj], sj)
             pivot = spread(cols[k + 1][tj], sj) - (element * element) * inverse
@@ -54,7 +74,7 @@
         for t in range(tk, groups):
             scaled[t] = cols[k][t] * inverse
         scaled[tk] = jnp.where(sub > sk, scaled[tk], 0.0)
-        for j in range(k + 1, BLK):
+        for j in range(k + 1, (k // HELD + 1) * HELD):
             tj, sj = divmod(j, 8)
             element = spread(cols[k][tj], sj)
             for t in range(tj, groups):
@@ -69,14 +89,6 @@
     return [[tile * roots[t] for tile in rows[t]] for t in range(groups)]
 
 
-def columns_of(tiles, offset):
-    cols = []
-    for j in range(BLK):
-        lane = jnp.full((8, 128), j, jnp.int32) + offset
-        cols.append([jnp.take_along_axis(tiles[t], lane, axis=1) if t >= j // 8 else None for t in range(BLK // 8)])
-    return cols
-
-
 def join(rows):
     return jnp.concatenate([jnp.concatenate(r, axis=1) for r in rows], axis=0)
 
@@ -86,14 +98,11 @@
 
     def step(p, low, first, end):
         base = pl.multiple_of(p * BLK, BLK)
-        lane = pl.multiple_of((p // 4) * 128, 128)
         span = slice(first * 128, end * 128)
-        block = [work[pl.ds(base + 8 * t, 8), pl.ds(lane, 128)] for t in range(groups)]
         rows = [[work[pl.ds(base + 8 * t, 8), c * 128 : c * 128 + 128] for c in range(first, end)] for t in range(groups)]
-        cols = columns_of(block, lax.rem(p, 4) * BLK)
         left = jnp.where(iota((256 - low, 128), 0) >= base + BLK - low, turned[low:, :], 0.0)[:, :BLK]
         work[low:, span] = work[low:, span] - nn(left, last[:, span])
-        rows = pivot_block(cols, rows)
+        rows = pivot_block(rows, lax.rem(p, 4) * BLK)
         for t in range(groups):
             for c in range(first, end):
                 work[pl.ds(base + 8 * t, 8), c * 128 : c * 128 + 128] = rows[t][c - first]
@@ -118,7 +127,8 @@
     half = jnp.where(down > across, 1.0, jnp.where(down == across, 0.5, 0.0)).astype(F32)
 
     def onward(x):
-        return -half * (excess + nt(x, x))
+        parts = halves(x)
+        return -half * (excess + split_product(parts, parts, 1))
 
     def more(state):
         return (state[1] > 1e-11) & (state[2] < 64)
@@ -128,11 +138,8 @@
         y = onward(x)
         return y, jnp.sum((y - x) * (y - x)), state[2] + 1
 
-    return lax.while_loop(more, body, (-half * excess, jnp.float32(1.0), jnp.int32(0)))[0]
-
-
-def sym(x):
-    return 0.5 * (x + x.T)
+    start = onward(onward(-half * excess))
+    return lax.while_loop(more, body, (start, jnp.float32(1.0), jnp.int32(0)))[0]
 
 
 def shrink(yt, gram, work, last, turned):
@@ -141,7 +148,7 @@
     work[:, 256:640] = yt
     factor(work, last, turned, (0, 5), (1, 5))
     qt = work[:, 256:640]
-    reduced = sym(nt(nn(qt, gram), qt))
+    reduced = nt(nn(qt, gram), qt)
     work[:, 0:256] = reduced
     work[:, 256:512] = eye
     factor(work, last, turned, (0, 3), (1, 4))
@@ -152,13 +159,20 @@
 
 
 def small(matrix, right):
-    tiles = right.shape[1] // 128
-    groups = BLK // 8
-    rows = [[right[8 * t : 8 * t + 8, c * 128 : c * 128 + 128] for c in range(tiles)] for t in range(groups)]
-    return join(pivot_block(columns_of([matrix[8 * t : 8 * t + 8] for t in range(groups)], 0), rows))
-
-
-def chain_kernel(packed_ref, sketch_ref, samples_ref, final_ref, residual_ref, work, last, turned, gram_ref, second_gram, coef_ref):
+    whole = jnp.concatenate([matrix, right], axis=1)
+    rows = [[whole[8 * t : 8 * t + 8, c * 128 : c * 128 + 128] for c in range(whole.shape[1] // 128)] for t in range(BLK // 8)]
+    return join(pivot_block(rows, 0))[:, 128:]
+
+
+def square_of(a, b):
+    return nt(a, jnp.concatenate([b, jnp.zeros((96, b.shape[1]), F32)], axis=0))
+
+
+def chain_kernel(packed_ref, sketch_hbm, samples_hbm, final_hbm, residual_hbm, work, last, turned, gram_ref, second_gram, data_ref, outs_ref, in_sems, out_sems):
+    sketch_in = pltpu.make_async_copy(sketch_hbm, data_ref.at[0:256], in_sems.at[0])
+    samples_in = pltpu.make_async_copy(samples_hbm, data_ref.at[256:384], in_sems.at[1])
+    sketch_in.start()
+    samples_in.start()
     index = 0
     for i in range(3):
         for j in range(i + 1):
@@ -172,12 +186,10 @@
     inner = (iota((384, 384), 0) < 320) & (iota((384, 384), 1) < 320)
     second_gram[...] = jnp.where(inner, gram_ref[...], 0.0)
     weights, keeper, reduced = shrink(yt, second_gram[...], work, last, turned)
-    corner = sym(nt(nn(keeper, reduced), keeper))
-    mixed = nn(weights, gram_ref[...])
-    side = mixed[:, 256:384]
-    tail = gram_ref[256:384, 256:384]
-    side = jnp.where(iota((256, 128), 1) < 64, pltpu.roll(side, 64, 1), 0.0)
-    tail = pltpu.roll(tail, 64, 1)[64:128]
+    corner = nt(nn(keeper, reduced), keeper)
+    side = pltpu.roll(nn(weights, gram_ref[:, 256:384]), 64, 1)
+    side = jnp.where(iota((256, 128), 1) < 64, side, 0.0)
+    tail = pltpu.roll(gram_ref[320:384, 256:384], 64, 1)
     tail = jnp.where(iota((64, 128), 1) < 64, tail, 0.0)
     second_gram[0:256, 0:256] = corner
     second_gram[0:256, 256:384] = side
@@ -185,45 +197,48 @@
     second_gram[256:320, 256:384] = tail
     second_gram[320:384, 256:384] = jnp.zeros((64, 128), F32)
     weights_two, keeper_two, reduced_two = shrink(second_gram[0:256, :], second_gram[...], work, last, turned)
-    shifted = jnp.where(iota((256, 128), 1) >= 64, pltpu.roll(weights_two[:, 256:384], 64, 1), 0.0)
+    late = pltpu.roll(weights_two[:, 256:384], 64, 1)
+    late = jnp.where(iota((256, 128), 1) >= 64, late, 0.0)
     whole = nn(weights_two[:, :256], weights)
-    whole = jnp.concatenate([whole[:, :256], whole[:, 256:] + shifted], axis=1)
-    coef_ref[0:256, :] = whole
-    spectrum = sym(nt(nn(keeper_two, reduced_two), keeper_two))
-    leading = spectrum[0:32, :]
-    block = nt(leading, jnp.concatenate([leading, jnp.zeros((96, 256), F32)], axis=0))
-    ut = small(block, leading)
-    padded = jnp.concatenate([ut, jnp.zeros((96, 256), F32)], axis=0)
-    block = nt(nn(ut, spectrum), padded)
-    block = 0.5 * (block + nt(ut, jnp.concatenate([nn(ut, spectrum), jnp.zeros((96, 256), F32)], axis=0)))
+    whole = jnp.concatenate([whole[:, :256], whole[:, 256:] + late], axis=1)
+    sketch_in.wait()
+    samples_in.wait()
+    weights_parts = halves(whole)
+    for i in range(4):
+        at = slice(i * 256, i * 256 + 256)
+        outs_ref[0:256, at] = split_product(weights_parts, halves(data_ref[:, at]), 0)
+    leading = nt(nn(keeper_two[0:32], reduced_two), keeper_two)
+    ut = small(square_of(leading, leading), leading)
+    kept = nn(ut, keeper_two)
     towards = nn(ut, whole)
-    scores = nn(towards, gram_ref[...])[:, 256:384]
-    both = small(block, jnp.concatenate([towards, scores], axis=1))
+    scores = nn(towards, gram_ref[:, 256:384])
+    both = small(square_of(nn(kept, reduced_two), kept), jnp.concatenate([towards, scores], axis=1))
     ident = (iota((128, 384), 1) == iota((128, 384), 0) + 256).astype(F32)
-    coef_ref[256:384, :] = ident - tn(both[:, 384:512], both[:, :384])
-
-
-    def columns(i, _):
-        at = pl.ds(pl.multiple_of(i * 256, 256), 256)
-        both = nn(coef_ref[:, 0:256], sketch_ref[:, at]) + nn(coef_ref[:, 256:384], samples_ref[:, at])
-        final_ref[:, at] = both[:256]
-        residual_ref[:, at] = both[256:]
-        return 0
-
-    lax.fori_loop(0, 4, columns, 0)
+    coef = halves(ident - tn(both[:, 384:512], both[:, :384]))
+    outs = [pltpu.make_async_copy(outs_ref.at[0:256], final_hbm, out_sems.at[4])]
+    outs[0].start()
+    for i in range(4):
+        at = slice(i * 256, i * 256 + 256)
+        outs_ref[256:384, at] = split_product(coef, halves(data_ref[:, at]), 0)
+        outs.append(pltpu.make_async_copy(outs_ref.at[256:384, at], residual_hbm.at[:, at], out_sems.at[i]))
+        outs[-1].start()
+    for copy in outs:
+        copy.wait()
 
 
 def chain(packed, sketch, samples):
-    vmem = pl.BlockSpec(memory_space=pltpu.VMEM)
+    vmem, anywhere = pl.BlockSpec(memory_space=pltpu.VMEM), pl.BlockSpec(memory_space=pl.ANY)
     square = pltpu.VMEM((384, 384), F32)
     return pl.pallas_call(
         chain_kernel,
         out_shape=(jax.ShapeDtypeStruct((256, 1024), F32), jax.ShapeDtypeStruct((128, 1024), F32)),
-        in_specs=[vmem] * 3,
-        out_specs=(vmem, vmem),
-        scratch_shapes=[pltpu.VMEM((256, 640), F32), pltpu.VMEM((BLK, 640), F32), pltpu.VMEM((256, 128), F32), square, square, square],
+        in_specs=[vmem, anywhere, anywhere],
+        out_specs=(anywhere, anywhere),
+        scratch_shapes=[
+            pltpu.VMEM((256, 640), F32), pltpu.VMEM((BLK, 640), F32), pltpu.VMEM((256, 128), F32), square, square,
+            pltpu.VMEM((384, 1024), F32), pltpu.VMEM((384, 1024), F32), pltpu.SemaphoreType.DMA((2,)), pltpu.SemaphoreType.DMA((5,)),
+        ],
     )(packed, sketch, samples)
-
 
 def spot():
     return tuple(lax.axis_index(name) for name in GRP_SUB)
@@ -234,32 +249,17 @@
     tile = None
     for i in range(4):
         host = owner_ref[at + i]
-        source = arrivals_ref[:, pl.ds(pl.multiple_of((host >> 2) * 128, 128), 128)]
-        turned = pltpu.roll(source, ((i - host) & 3) * 32, 1)
+        source = arrivals_ref[host // 4]
+        run = jnp.full((8, 128), host % 4, jnp.int32)
+        turned = source
+        for q in range(1, 4):
+            turned = jnp.where(run == (i + 4 - q) % 4, pltpu.roll(source, q * 32, 1), turned)
         tile = turned if i == 0 else jnp.where(quarter == i, turned, tile)
     return tile
 
 
-def place_kernel(owner_ref, arrivals_ref, placed_ref):
-    def block(j, _):
-        for v in range(8):
-            placed_ref[j, :, v * 128 : v * 128 + 128] = place_tile(owner_ref, arrivals_ref, j * 32 + v * 4)
-        return 0
-
-    lax.fori_loop(0, 16, block, 0)
-
-
-def place(owner, arrivals):
-    return pl.pallas_call(
-        place_kernel,
-        out_shape=jax.ShapeDtypeStruct((16, 8, 1024), F32),
-        in_specs=[pl.BlockSpec(memory_space=pltpu.SMEM), pl.BlockSpec(memory_space=pltpu.VMEM)],
-        out_specs=pl.BlockSpec(memory_space=pltpu.VMEM),
-    )(owner, arrivals)
-
-
-def collect_kernel(slot_ref, placed, sketch_ref, total_ref, samples_ref,
-                   landed, part, twin, half, plane, piece, column, share, whole,
+def collect_kernel(owner_ref, slot_ref, arrivals_ref, sketch_ref, total_ref, samples_ref,
+                   placed, landed, part, twin, half, plane, piece, column, share, whole,
                    move_send, move_recv, twin_sems, plane_send, plane_recv, column_send, column_recv, share_send, share_recv, back_send, back_recv):
     y_hi, x, core, y_lo, z = spot()
     me_sub = y_lo * 8 + z
@@ -288,12 +288,24 @@
         pl.semaphore_signal(barrier, inc=1, device_id=in_sub(lax.rem(me_sub + s, 16)), device_id_type=MESH)
         pl.semaphore_signal(barrier, inc=1, device_id=in_plane(lax.rem(me + s, 16)), device_id_type=MESH)
 
-    landed[me_sub] = placed[me_sub]
-    pl.semaphore_wait(barrier, 31)
+    def place(peer):
+        def step(i, _):
+            for v in range(4):
+                tile = place_tile(owner_ref, arrivals_ref, peer * 32 + i * 16 + v * 4)
+                placed[peer, :, pl.ds(pl.multiple_of(i * 512 + v * 128, 128), 128)] = tile
+            return 0
+
+        lax.fori_loop(0, 2, step, 0)
+
     moves = []
     for s in (8, 4, 12, 3, 5, 11, 13, 2, 6, 10, 14, 1, 7, 9, 15):
         peer = lax.rem(me_sub + s, 16)
+        place(peer)
+        if not moves:
+            pl.semaphore_wait(barrier, 31)
         moves.append(send(placed.at[peer], landed.at[me_sub], move_send.at[s], move_recv.at[s], in_sub(peer)))
+    place(me_sub)
+    landed[me_sub] = placed[me_sub]
 
     def put(index, block):
         rows = block.reshape(16, 8, 128)
@@ -361,16 +373,16 @@
     return pl.pallas_call(
         collect_kernel,
         out_shape=(jax.ShapeDtypeStruct((768, 128), F32), jax.ShapeDtypeStruct((128, 1024), F32)),
-        in_specs=[vmem, vmem, vmem],
+        in_specs=[pl.BlockSpec(memory_space=pltpu.SMEM), vmem, vmem, vmem],
         out_specs=(vmem, vmem),
         scratch_shapes=[
-            pltpu.VMEM((16, 8, 1024), F32), pltpu.VMEM((2, 16, 24, 128), F32),
+            pltpu.VMEM((16, 8, 1024), F32), pltpu.VMEM((16, 8, 1024), F32), pltpu.VMEM((2, 16, 24, 128), F32),
             pltpu.VMEM((16, 24, 128), F32), pltpu.VMEM((16, 24, 128), F32), pltpu.VMEM((16, 24, 128), F32),
             pltpu.VMEM((24, 128), F32), pltpu.VMEM((8, 24, 128), F32), pltpu.VMEM((24, 128), F32), pltpu.VMEM((2, 16, 24, 128), F32),
             dma((16,)), dma((16,)), dma((2,)), dma((16,)), dma((16,)), dma((8,)), dma((8,)), dma((16,)), dma((16,)), dma((16,)), dma((16,)),
         ],
         compiler_params=pltpu.CompilerParams(collective_id=0, has_side_effects=True),
-    )(slot, place(owner, arrivals), sketch)
+    )(owner, slot, arrivals.reshape(8, 128, 128).transpose(1, 0, 2), sketch)
 
 
 def local(arrivals, sketch, owner, slot):

time: 105 us -> 96.1 us (0.915)
  Pallas kernels: 104 us -> 95.2 us
    pallas_call x1, Pallas kernels: 51 us -> 45.4 us  [chain(): pl.pallas_call(chain_kernel, out_shape=(jax.ShapeDtypeStruct((256, 1024),...]
    pallas_call x1 -> x0, Pallas kernels: 4.37 us -> none  [place(): pl.pallas_call(place_kernel, out_shape=jax.ShapeDtypeStruct((16, 8, 1024)...]
    pallas_call x1, Pallas kernels: 48.6 us -> 49.7 us  [collect(): pl.pallas_call(collect_kernel, out_shape=(jax.ShapeDtypeStruct((768, 128)...]
where the time goes in v4:
time: 96.1 us; the launch traced here: 96 us
  Pallas kernels  95.2 us (99%)
    pallas_call x1, Pallas kernels, collect(): pl.pallas_call(collect_kernel, out_shape=(jax.ShapeDtypeStruct((768, 128)...  49.7 us
    pallas_call x1, Pallas kernels, chain(): pl.pallas_call(chain_kernel, out_shape=(jax.ShapeDtypeStruct((256, 1024),...  45.4 us

profile of v4, /device:TPU:1, one launch (start us, length us, event | category | flops | bytes accessed | tf_op | source)
XLA Modules:
  0.0 96.0 jit_solution(10638547882963257256)
XLA Ops:
  0.6 49.7 %shard_map.59 = (f32[768,128]{1,0:T(8,128)}, f32[128,1024]{1,0:T(8,128)}) custom-call(s32[512]{0:T(512)} %owner_ref.1, s32[1,128]{1,0:T(1,128)} %bitcast.5, f32[128,8,128]{2,1,0:T(8,128)} %bitcast.4, f32[256,1024]{1,0:T(8,128)} %sketch_hbm.1), custom_call_target="tpu_custom_call" | custom-call | tf_op jit(solution)/shard_map/pallas_call | solution.py:373
  50.4 45.4 %shard_map.60 = (f32[256,1024]{1,0:T(8,128)}, f32[128,1024]{1,0:T(8,128)}) custom-call(f32[768,128]{1,0:T(8,128)} %get-tuple-element.4.packed_ref, f32[256,1024]{1,0:T(8,128)} %sketch_hbm.1, f32[128,1024]{1,0:T(8,128)} %get-tuple-element.5.samples_hbm), custom_call_target="tpu_custom_call" | custom-call | tf_op jit(solution)/shard_map/pallas_call | solution.py:232

commit v5 on v4

--- a/solution.py
+++ b/solution.py
@@ -96,30 +96,38 @@
 def factor(work, last, turned, early, late):
     groups = BLK // 8
 
-    def step(p, low, first, end):
-        base = pl.multiple_of(p * BLK, BLK)
+    def half(low, first, end):
         span = slice(first * 128, end * 128)
-        rows = [[work[pl.ds(base + 8 * t, 8), c * 128 : c * 128 + 128] for c in range(first, end)] for t in range(groups)]
-        left = jnp.where(iota((256 - low, 128), 0) >= base + BLK - low, turned[low:, :], 0.0)[:, :BLK]
-        work[low:, span] = work[low:, span] - nn(left, last[:, span])
-        rows = pivot_block(rows, lax.rem(p, 4) * BLK)
-        for t in range(groups):
-            for c in range(first, end):
-                work[pl.ds(base + 8 * t, 8), c * 128 : c * 128 + 128] = rows[t][c - first]
-        panel = join(rows)
-        last[:, span] = panel
-        turned[low:, 0:BLK] = panel[:, low - first * 128 : 256 - first * 128].T
-
-        @pl.when(p < 7)
-        def _():
-            below = pl.ds(base + BLK, BLK)
-            work[below, span] = work[below, span] - nn(turned[below, 0:BLK], panel)
-        return 0
-
-    last[...] = jnp.zeros_like(last)
-    turned[...] = jnp.zeros_like(turned)
-    lax.fori_loop(0, 4, lambda p, _: step(p, 0, *early), 0)
-    lax.fori_loop(4, 8, lambda p, _: step(p, 128, *late), 0)
+        last[...] = jnp.zeros_like(last)
+        turned[...] = jnp.zeros_like(turned)
+
+        def step(p, _):
+            base = pl.multiple_of(p * BLK, BLK)
+            at = pl.multiple_of(low + base, BLK)
+            rows = [[work[pl.ds(at + 8 * t, 8), c * 128 : c * 128 + 128] for c in range(first, end)] for t in range(groups)]
+            left = jnp.where(iota((128, 128), 0) >= base + BLK, turned[...], 0.0)[:, :BLK]
+            work[low : low + 128, span] = work[low : low + 128, span] - nn(left, last[:, span])
+            rows = pivot_block(rows, base)
+            for t in range(groups):
+                for c in range(first, end):
+                    work[pl.ds(at + 8 * t, 8), c * 128 : c * 128 + 128] = rows[t][c - first]
+            panel = join(rows)
+            last[:, span] = panel
+            turned[:, 0:BLK] = panel[:, :128].T
+
+            @pl.when(p < 3)
+            def _():
+                below = pl.ds(at + BLK, BLK)
+                work[below, span] = work[below, span] - nn(turned[pl.ds(base + BLK, BLK), 0:BLK], panel)
+            return 0
+
+        lax.fori_loop(0, 4, step, 0)
+
+    half(0, *early)
+    first, end = max(early[0], late[0]), min(early[1], late[1])
+    span = slice(first * 128, end * 128)
+    work[128:256, span] = work[128:256, span] - tn(work[0:128, 128:256], work[0:128, span])
+    half(128, *late)
 
 
 def near_identity_root(excess):
@@ -235,10 +243,14 @@
         in_specs=[vmem, anywhere, anywhere],
         out_specs=(anywhere, anywhere),
         scratch_shapes=[
-            pltpu.VMEM((256, 640), F32), pltpu.VMEM((BLK, 640), F32), pltpu.VMEM((256, 128), F32), square, square,
+            pltpu.VMEM((256, 640), F32), pltpu.VMEM((BLK, 640), F32), pltpu.VMEM((128, 128), F32), square, square,
             pltpu.VMEM((384, 1024), F32), pltpu.VMEM((384, 1024), F32), pltpu.SemaphoreType.DMA((2,)), pltpu.SemaphoreType.DMA((5,)),
         ],
     )(packed, sketch, samples)
+
+PLANE = ((2, 2), (2, 1), (2, 3), (1, 2), (3, 2), (2, 0), (0, 2), (1, 1), (1, 3), (3, 1), (3, 3), (1, 0), (3, 0), (0, 1), (0, 3))
+COLUMN = (4, 3, 5, 2, 6, 1, 7)
+
 
 def spot():
     return tuple(lax.axis_index(name) for name in GRP_SUB)
@@ -258,19 +270,22 @@
     return tile
 
 
-def collect_kernel(owner_ref, slot_ref, arrivals_ref, sketch_ref, total_ref, samples_ref,
-                   placed, landed, part, twin, half, plane, piece, column, share, whole,
+def collect_kernel(owner_ref, slot_ref, arrivals_ref, sketch_hbm, total_ref, samples_hbm,
+                   sketch_ref, samples_ref, local_sems, placed, landed, part, twin, half, plane, piece, column, share, whole,
                    move_send, move_recv, twin_sems, plane_send, plane_recv, column_send, column_recv, share_send, share_recv, back_send, back_recv):
     y_hi, x, core, y_lo, z = spot()
     me_sub = y_lo * 8 + z
-    me = (y_hi * 2 + y_lo) * 4 + x
+    y = y_hi * 2 + y_lo
+    me = y * 4 + x
+    sketch_in = pltpu.make_async_copy(sketch_hbm, sketch_ref, local_sems.at[0])
+    sketch_in.start()
 
     def in_sub(j):
         return (y_hi, x, core, j // 8, lax.rem(j, 8))
 
-    def in_plane(q):
-        y = q // 4
-        return (y // 2, lax.rem(q, 4), core, lax.rem(y, 2), z)
+    def over(step):
+        to_y, to_x = lax.rem(y + step[0], 4), lax.rem(x + step[1], 4)
+        return (to_y // 2, to_x, core, lax.rem(to_y, 2), z), to_y * 4 + to_x
 
     def in_column(k):
         return (y_hi, x, core, y_lo, k)
@@ -286,7 +301,8 @@
     pl.semaphore_signal(barrier, inc=1, device_id=other, device_id_type=MESH)
     for s in range(1, 16):
         pl.semaphore_signal(barrier, inc=1, device_id=in_sub(lax.rem(me_sub + s, 16)), device_id_type=MESH)
-        pl.semaphore_signal(barrier, inc=1, device_id=in_plane(lax.rem(me + s, 16)), device_id_type=MESH)
+    for step in PLANE:
+        pl.semaphore_signal(barrier, inc=1, device_id=over(step)[0], device_id_type=MESH)
 
     def place(peer):
         def step(i, _):
@@ -313,6 +329,7 @@
             at = index * 16 + r
             part[at // 48, (at % 48) // 3, (at % 3) * 8 : (at % 3) * 8 + 8, :] = rows[r]
 
+    sketch_in.wait()
     put(0, nt(sketch_ref[0:128, :], sketch_ref[0:128, :]))
     put(1, nt(sketch_ref[128:256, :], sketch_ref[0:128, :]))
     put(2, nt(sketch_ref[128:256, :], sketch_ref[128:256, :]))
@@ -320,6 +337,8 @@
         copy.wait_recv()
     pick = (iota((128, 128), 0) == slot_ref[...]).astype(F32)
     samples_ref[...] = tn(pick, landed[...].reshape(128, 1024))
+    samples_out = pltpu.make_async_copy(samples_ref, samples_hbm, local_sems.at[1])
+    samples_out.start()
     put(3, nt(samples_ref[...], sketch_ref[0:128, :]))
     put(4, nt(samples_ref[...], sketch_ref[128:256, :]))
     put(5, nt(samples_ref[...], samples_ref[...]))
@@ -329,19 +348,18 @@
     half[...] = part[core] + twin[...]
 
     scattered = []
-    for s in range(1, 16):
-        peer = lax.rem(me + s, 16)
-        scattered.append(send(half.at[peer], plane.at[s], plane_send.at[s], plane_recv.at[s], in_plane(peer)))
+    for i, step in enumerate(PLANE):
+        device, peer = over(step)
+        scattered.append(send(half.at[peer], plane.at[i], plane_send.at[i], plane_recv.at[i], device))
     total = half[me]
-    for s in range(1, 16):
-        scattered[s - 1].wait_recv()
-        total = total + plane[s]
+    for i in range(15):
+        scattered[i].wait_recv()
+        total = total + plane[i]
     piece[...] = total
 
     spread_out = []
-    for s in range(1, 8):
-        peer = lax.rem(z + s, 8)
-        spread_out.append(send(piece, column.at[z], column_send.at[s], column_recv.at[s], in_column(peer)))
+    for s in COLUMN:
+        spread_out.append(send(piece, column.at[z], column_send.at[s], column_recv.at[s], in_column(lax.rem(z + s, 8))))
     column[z] = piece[...]
     for copy in spread_out:
         copy.wait_recv()
@@ -351,31 +369,33 @@
     share[...] = total
 
     gathered = []
-    for s in range(1, 16):
-        peer = lax.rem(me + s, 16)
-        gathered.append(send(share, whole.at[core, me], share_send.at[s], share_recv.at[s], in_plane(peer)))
+    for i, step in enumerate(PLANE):
+        gathered.append(send(share, whole.at[core, me], share_send.at[i], share_recv.at[i], over(step)[0]))
     whole[core, me] = share[...]
-    back = [send(share, whole.at[core, me], back_send.at[0], back_recv.at[0], other)]
-    for s in range(1, 16):
-        gathered[s - 1].wait_recv()
-        source = lax.rem(me + 16 - s, 16)
-        back.append(send(whole.at[core, source], whole.at[core, source], back_send.at[s], back_recv.at[s], other))
+    back = [send(share, whole.at[core, me], back_send.at[15], back_recv.at[15], other)]
+    for i in range(14, -1, -1):
+        step = PLANE[i]
+        gathered[i].wait_recv()
+        source = over((4 - step[0], 4 - step[1]))[1]
+        back.append(send(whole.at[core, source], whole.at[core, source], back_send.at[i], back_recv.at[i], other))
     for copy in back:
         copy.wait_recv()
     total_ref[...] = whole[...].reshape(768, 128)
     for copy in moves + [first] + scattered + spread_out + gathered + back:
         copy.wait_send()
+    samples_out.wait()
 
 
 def collect(owner, slot, arrivals, sketch):
     dma = pltpu.SemaphoreType.DMA
-    vmem = pl.BlockSpec(memory_space=pltpu.VMEM)
+    vmem, anywhere = pl.BlockSpec(memory_space=pltpu.VMEM), pl.BlockSpec(memory_space=pl.ANY)
     return pl.pallas_call(
         collect_kernel,
         out_shape=(jax.ShapeDtypeStruct((768, 128), F32), jax.ShapeDtypeStruct((128, 1024), F32)),
-        in_specs=[pl.BlockSpec(memory_space=pltpu.SMEM), vmem, vmem, vmem],
-        out_specs=(vmem, vmem),
+        in_specs=[pl.BlockSpec(memory_space=pltpu.SMEM), vmem, vmem, anywhere],
+        out_specs=(vmem, anywhere),
         scratch_shapes=[
+            pltpu.VMEM((256, 1024), F32), pltpu.VMEM((128, 1024), F32), dma((2,)),
             pltpu.VMEM((16, 8, 1024), F32), pltpu.VMEM((16, 8, 1024), F32), pltpu.VMEM((2, 16, 24, 128), F32),
             pltpu.VMEM((16, 24, 128), F32), pltpu.VMEM((16, 24, 128), F32), pltpu.VMEM((16, 24, 128), F32),
             pltpu.VMEM((24, 128), F32), pltpu.VMEM((8, 24, 128), F32), pltpu.VMEM((24, 128), F32), pltpu.VMEM((2, 16, 24, 128), F32),

time: 96.1 us -> 94.5 us (0.983)
  Pallas kernels: 95.2 us -> 93.6 us
    pallas_call x1, Pallas kernels: 49.7 us -> 48.2 us  [collect(): pl.pallas_call(collect_kernel, out_shape=(jax.ShapeDtypeStruct((768, 128)...]
where the time goes in v5:
time: 94.5 us; the launch traced here: 94.4 us
  Pallas kernels  93.6 us (99%)
    pallas_call x1, Pallas kernels, collect(): pl.pallas_call(collect_kernel, out_shape=(jax.ShapeDtypeStruct((768, 128)...  48.2 us
    pallas_call x1, Pallas kernels, chain(): pl.pallas_call(chain_kernel, out_shape=(jax.ShapeDtypeStruct((256, 1024),...  45.3 us

profile of v5, /device:TPU:1, one launch (start us, length us, event | category | flops | bytes accessed | tf_op | source)
XLA Modules:
  0.0 94.4 jit_solution(18284431276488749035)
XLA Ops:
  0.6 48.2 %shard_map.59 = (f32[768,128]{1,0:T(8,128)}, f32[128,1024]{1,0:T(8,128)}) custom-call(s32[512]{0:T(512)} %owner_ref.1, s32[1,128]{1,0:T(1,128)} %bitcast.5, f32[128,8,128]{2,1,0:T(8,128)} %bitcast.4, f32[256,1024]{1,0:T(8,128)} %sketch_hbm.3), custom_call_target="tpu_custom_call" | custom-call | tf_op jit(solution)/shard_map/pallas_call | solution.py:392
  48.9 45.3 %shard_map.60 = (f32[256,1024]{1,0:T(8,128)}, f32[128,1024]{1,0:T(8,128)}) custom-call(f32[768,128]{1,0:T(8,128)} %get-tuple-element.4.packed_ref, f32[256,1024]{1,0:T(8,128)} %sketch_hbm.3, f32[128,1024]{1,0:T(8,128)} %get-tuple-element.5.samples_hbm), custom_call_target="tpu_custom_call" | custom-call | tf_op jit(solution)/shard_map/pallas_call | solution.py:240
